TPU v7x, 768 devices: a whole 4x8x12 slice. The times are simulated.
768 devices in a mesh: lat: 12 (over z), rad: 64 (over x, y, core).
Axes of the slice: x: 4, y: 8, z: 12, core: 2. Of those that a mesh axis runs over, the one named last changes fastest.
Arguments:
- positions: float32 [98304, 3, 128], P(('lat', 'rad')), may hold values from 0 to 1
- fields: bfloat16 [98304, 16, 128], P(('lat', 'rad')), may hold values from -6 to 6
- velocity: float32 [81, 196608], P(None, ('lat', 'rad')), may hold values from -3 to 3
- counts: int32 [768], P(('lat', 'rad')), may hold values from 1 to 128, as said below
- elements: int32 [3, 98304], P(None, ('lat', 'rad')), may hold values from 0 to 255
- routes: int32 [2, 98304], P(None, ('lat', 'rad')), may hold values from 0 to 191
Outputs:
- moved: float32 [147456, 3, 128], P(('lat', 'rad'))
- projected: float32 [27, 16, 196608], P(None, None, ('lat', 'rad'))
Inputs may be any that keep to these rules, and one draw needn't show every extreme that they name: counts[d] is at most 128 and equals 128 on some device.
All inputs are finite; a program needn't handle non-finite values.
Results may differ from a plain program's by a relative error of at most 0.0003.
Values sent between devices are 32-bit elements; how exact they have to be, the bound alone decides.
A program may use at most 32 MiB of HBM per device.

v0:
```python
import jax
import jax.numpy as jnp
from jax import lax
from jax.sharding import PartitionSpec as P

time_step = 0.4
exact = lax.Precision.HIGHEST


def passed_along(x, axis, by):
    size = lax.axis_size(axis)
    return lax.ppermute(x, axis, [(i, (i + by) % size) for i in range(size)])


def lagrange(coord):
    first_node = 2.0 * (coord - 0.5) * (coord - 1.0)
    middle_node = -4.0 * coord * (coord - 1.0)
    last_node = 2.0 * coord * (coord - 0.5)
    return jnp.stack([first_node, middle_node, last_node], axis=0)


def basis(points):
    along_x = lagrange(points[:, 0, :])
    along_y = lagrange(points[:, 1, :])
    along_z = lagrange(points[:, 2, :])
    table = along_x[:, None, None] * along_y[None, :, None] * along_z[None, None, :]
    return jnp.moveaxis(table.reshape(27, points.shape[0], points.shape[2]), 0, 1)


def speed(columns, points):
    coefficients = columns.T.reshape(points.shape[0], 3, 27)
    return jnp.einsum("scn,snb->scb", coefficients, basis(points), precision=exact)


def place_rows(target, valid, number):
    matches = (target[:, None] == jnp.arange(number, dtype=jnp.int32)[None, :]) & valid[:, None]
    present = jnp.any(matches, axis=0)
    source = jnp.sum(
        jnp.where(matches, jnp.arange(target.shape[0], dtype=jnp.int32)[:, None], 0), axis=0
    )
    return (source, present)


def arrange(cargo, source, present):
    result = []
    for member in cargo:
        picked = jnp.take(member, source, axis=0)
        layout = (present.shape[0],) + (1,) * (member.ndim - 1)
        result.append(jnp.where(present.reshape(layout), picked, jnp.zeros_like(picked)))
    return tuple(result)


def migrate(cargo, rad_count, capacity):
    kinds = tuple((member.dtype for member in cargo))
    shaped = tuple(
        (
            member.astype(jnp.float32).reshape((3, rad_count, capacity) + member.shape[1:])
            for member in cargo
        )
    )
    crossed = lax.all_to_all(shaped, "rad", split_axis=1, concat_axis=1, tiled=True)
    sheets = []
    for sheet_number in range(3):
        portion = tuple((member[sheet_number] for member in crossed))
        if sheet_number != 1:
            portion = passed_along(portion, "lat", sheet_number - 1)
        sheets.append(portion)
    moved = tuple(
        (
            jnp.stack([sheets[sheet_number][member_index] for sheet_number in range(3)])
            for member_index in range(len(cargo))
        )
    )
    result = []
    for member, kind in zip(moved, kinds):
        flat = member.reshape((3 * rad_count * capacity,) + member.shape[3:])
        result.append(flat.astype(jnp.int32) if kind == jnp.int32 else flat)
    return tuple(result)


def block_sums(points, carried):
    shapes = basis(points)
    moments = jnp.einsum("snb,sfb->snf", shapes, carried, precision=exact)
    return (moments, jnp.sum(shapes * shapes, axis=2))


def per_device(positions, fields, velocity, counts, elements, routes):
    rad_count = lax.axis_size("rad")
    blocks = positions.shape[0]
    capacity = max(1, 2 * blocks // (3 * rad_count))
    places = 3 * rad_count * capacity
    owned = velocity.shape[1]
    home_valid = jnp.arange(blocks, dtype=jnp.int32) < counts[0]
    first_speed = speed(jnp.take(velocity, elements[0], axis=1), positions)
    midway = positions + 0.5 * time_step * first_speed
    source, present = place_rows(routes[0], home_valid, places)
    wide_fields = fields.astype(jnp.float32)
    labels = jnp.stack([home_valid.astype(jnp.int32), elements[1], routes[1], elements[2]], axis=1)
    pairs = jnp.stack([positions, midway], axis=1)
    labels, pairs, carried = migrate(
        arrange((labels, pairs, wide_fields), source, present), rad_count, capacity
    )
    mid_valid = labels[:, 0] > 0
    second_speed = speed(jnp.take(velocity, labels[:, 1], axis=1), pairs[:, 1])
    landed = pairs[:, 0] + time_step * second_speed
    source, present = place_rows(labels[:, 2], mid_valid, places)
    tags = jnp.stack([mid_valid.astype(jnp.int32), labels[:, 3]], axis=1)
    tags, arrived, carried = migrate(
        arrange((tags, landed, carried), source, present), rad_count, capacity
    )
    moments, weights_sum = block_sums(arrived, carried)
    final_valid = tags[:, 0] > 0
    hits = (
        (tags[:, 1][:, None] == jnp.arange(owned, dtype=jnp.int32)[None, :]) & final_valid[:, None]
    ).astype(jnp.float32)
    totals = jnp.einsum("se,snf->nfe", hits, moments, precision=exact)
    weights = jnp.einsum("se,sn->ne", hits, weights_sum, precision=exact)
    projected = totals / (1.0 + weights[:, None, :])
    return (arrived, projected)


def solution(mesh):
    in_specs = (
        P(("lat", "rad"), None, None),
        P(("lat", "rad"), None, None),
        P(None, ("lat", "rad")),
        P(("lat", "rad")),
        P(None, ("lat", "rad")),
        P(None, ("lat", "rad")),
    )
    out_specs = (P(("lat", "rad"), None, None), P(None, None, ("lat", "rad")))
    return jax.shard_map(
        per_device, mesh=mesh, in_specs=in_specs, out_specs=out_specs, check_vma=False
    )
```

profile of v0, /device:TPU:1, one launch (start us, length us, event | category | flops | bytes accessed | tf_op | source)
XLA Modules:
  0.0 222.7 jit_solution(16234352918057904376)
XLA Ops:
  1.4 0.8 slice_bitcast_fusion.15
  2.9 0.7 gather_fusion
  3.6 1.2 fusion.23
  4.8 14.5 %all-to-all-start = ((f32[3,64,1,4]{3,2,0,1:T(1,128)}), f32[3,64,1,4]{3,2,0,1:T(1,128)S(1)}, u32[]{:S(2)}, u32[]{:S(2)}) async-start(f32[3,64,1,4]{3,2,0,1:T(1,128)} %fusion.23), calls=%async_computation | async-start | bytes 196608 | tf_op jit(solution)/shard_map/all_to_all | solution.py:61
  19.4 0.7 fusion.30
  20.1 0.7 compare_and_fusion
  20.8 1.0 multiply_bitcast_fusion.26
  22.0 0.6 gather_fusion.1
  23.2 2.7 %fusion.12 = f32[128,1,3,128]{3,2,0,1:T(4,128)S(1)} fusion(f32[128,3,27]{2,1,0:T(4,128)S(1)} %reshape.995, f32[128,27,128]{2,0,1:T(8,128)S(1)} %bitcast.171, f32[128,3,128]{2,0,1:T(8,128)S(1)} %copy-done), kind=kOutput, calls=%fused_computation.24 | convolution fusion | flops 16023552 | bytes 2204160 | tf_op jit(solution)/shard_map/scn,snb->scb/dot_general | solution.py:32
  26.0 1.2 gather_fusion.2
  27.2 1.3 fusion.15
  28.6 0.9 gather_fusion.5
  29.7 10.3 %all-to-all-start.1 = ((f32[3,64,1,2,3,128]{5,3,4,2,0,1:T(2,128)}), f32[3,64,1,2,3,128]{5,3,4,2,0,1:T(2,128)S(1)}, u32[]{:S(2)}, u32[]{:S(2)}) async-start(f32[3,64,1,2,3,128]{5,3,4,2,0,1:T(2,128)} %fusion.15), calls=%async_computation.1 | async-start | bytes 1179648 | tf_op jit(solution)/shard_map/all_to_all | solution.py:61
  40.1 1.9 collective-permute-start.1
  42.0 11.3 %collective-permute-start = (f32[64,1,4]{2,0,1:T(8,128)S(1)}, f32[64,1,4]{2,0,1:T(8,128)S(1)}, u32[]{:S(2)}, u32[]{:S(2)}) collective-permute-start(f32[64,1,4]{2,0,1:T(8,128)S(1)} %bitcast.194), channel_id=1, source_target_pairs={{0,704},{64,0},{128,64},{192,128},{256,192},{320,256},{384,320},{4... | collective-permute-start | bytes 3080 | tf_op jit(solution)/shard_map/ppermute | solution.py:12
  53.3 0.6 select_select_fusion.1
  53.9 1.3 copy.365
  56.2 2.4 %all-to-all-done.1 = f32[3,64,1,2,3,128]{5,3,4,2,0,1:T(2,128)S(1)} async-done(((f32[3,64,1,2,3,128]{5,3,4,2,0,1:T(2,128)}), f32[3,64,1,2,3,128]{5,3,4,2,0,1:T(2,128)S(1)}, u32[]{:S(2)}, u32[]{:S(2)}) %all-to-all-start.1) | async-done | bytes 589856 | tf_op jit(solution)/shard_map/all_to_all | solution.py:61
  58.7 8.2 %all-to-all-start.3 = ((f32[3,64,1,16,128]{4,3,0,2,1:T(8,128)}), f32[3,64,1,16,128]{4,3,0,2,1:T(8,128)S(1)}, u32[]{:S(2)}, u32[]{:S(2)}) async-start(f32[3,64,1,16,128]{4,3,0,2,1:T(8,128)} %copy.365), calls=%async_computation.3 | async-start | bytes 3145728 | tf_op jit(solution)/shard_map/all_to_all | solution.py:61
  66.9 0.7 gather_fusion.3
  68.0 0.7 gather_fusion.7
  68.7 0.5 copy.375
  69.4 1.9 collective-permute-start.3
  71.4 9.6 %collective-permute-start.2 = (f32[64,1,2,3,128]{4,2,3,0,1:T(2,128)S(1)}, f32[64,1,2,3,128]{4,2,3,0,1:T(2,128)S(1)}, u32[]{:S(2)}, u32[]{:S(2)}) collective-permute-start(f32[64,1,2,3,128]{4,2,3,0,1:T(2,128)S(1)} %get-tuple-element.10), channel_id=1, source_target_pairs={{0,704},{64,0},{128,64},{192,128},{256,192},{320,256},{384,320},{4... | collective-permute-start | bytes 589832 | tf_op jit(solution)/shard_map/ppermute | solution.py:12
  80.9 0.7 select_convert_fusion
  81.6 2.0 collective-permute-done.3
  83.6 0.9 collective-permute-done.2
  84.5 0.3 pad_maximum_fusion.2
  85.2 0.3 broadcast_multiply_fusion.1
  85.5 4.0 %fusion.2 = f32[192,3,128]{2,1,0:T(4,128)S(1)} fusion(f32[192,3,27]{2,1,0:T(4,128)S(1)} %reshape.996, f32[192,27,128]{2,0,1:T(8,128)S(1)} %bitcast.170), kind=kOutput, calls=%fused_computation.10 | convolution fusion | flops 23887872 | bytes 3011328 | tf_op jit(solution)/shard_map/scn,snb->scb/dot_general | solution.py:32
  89.5 17.2 %all-to-all-done.3 = f32[3,64,1,16,128]{4,3,0,2,1:T(8,128)S(1)} async-done(((f32[3,64,1,16,128]{4,3,0,2,1:T(8,128)}), f32[3,64,1,16,128]{4,3,0,2,1:T(8,128)S(1)}, u32[]{:S(2)}, u32[]{:S(2)}) %all-to-all-start.3) | async-done | bytes 1572896 | tf_op jit(solution)/shard_map/all_to_all | solution.py:61
  106.6 6.1 %all-to-all-start.5 = ((f32[3,64,1,2]{0,3,2,1:T(2,128)}), f32[3,64,1,2]{0,3,2,1:T(2,128)S(1)}, u32[]{:S(2)}, u32[]{:S(2)}) async-start(f32[3,64,1,2]{0,3,2,1:T(2,128)} %select_convert_fusion), calls=%async_computation.5 | async-start | bytes 131072 | tf_op jit(solution)/shard_map/all_to_all | solution.py:61
  112.7 1.1 slice_bitcast_fusion.5
  113.9 1.9 collective-permute-start.7
  115.8 9.4 %collective-permute-start.6 = (f32[64,1,16,128]{3,2,0,1:T(8,128)}, f32[64,1,16,128]{3,2,0,1:T(8,128)}, u32[]{:S(2)}, u32[]{:S(2)}) collective-permute-start(f32[64,1,16,128]{3,2,0,1:T(8,128)} %get-tuple-element.7), channel_id=1, source_target_pairs={{0,704},{64,0},{128,64},{192,128},{256,192},{320,256},{384,320},{4... | collective-permute-start | bytes 1572872 | tf_op jit(solution)/shard_map/ppermute | solution.py:12
  125.4 0.9 gather_fusion.4
  126.3 1.3 broadcast_select_fusion.1
  127.6 10.6 %all-to-all-start.2 = ((f32[3,64,1,3,128]{4,2,3,0,1:T(1,128)}), f32[3,64,1,3,128]{4,2,3,0,1:T(1,128)S(1)}, u32[]{:S(2)}, u32[]{:S(2)}) async-start(f32[3,64,1,3,128]{4,2,3,0,1:T(1,128)} %broadcast_select_fusion.1), calls=%async_computation.2 | async-start | bytes 589824 | tf_op jit(solution)/shard_map/all_to_all | solution.py:61
  138.2 1.1 pad_maximum_fusion
  139.4 0.9 gather_fusion.6
  140.3 0.6 select_select_fusion
  140.9 1.3 copy.368
  142.1 8.7 %all-to-all-done.2 = f32[3,64,1,3,128]{4,2,3,0,1:T(1,128)S(1)} async-done(((f32[3,64,1,3,128]{4,2,3,0,1:T(1,128)}), f32[3,64,1,3,128]{4,2,3,0,1:T(1,128)S(1)}, u32[]{:S(2)}, u32[]{:S(2)}) %all-to-all-start.2) | async-done | bytes 294944 | tf_op jit(solution)/shard_map/all_to_all | solution.py:61
  150.8 6.1 %all-to-all-start.4 = ((f32[3,64,1,16,128]{4,3,0,2,1:T(8,128)}), f32[3,64,1,16,128]{4,3,0,2,1:T(8,128)S(1)}, u32[]{:S(2)}, u32[]{:S(2)}) async-start(f32[3,64,1,16,128]{4,3,0,2,1:T(8,128)} %copy.368), calls=%async_computation.4 | async-start | bytes 3145728 | tf_op jit(solution)/shard_map/all_to_all | solution.py:61
  157.2 1.9 collective-permute-start.11
  159.2 4.6 %collective-permute-start.10 = (f32[64,1,2]{0,2,1:T(2,128)S(1)}, f32[64,1,2]{0,2,1:T(2,128)S(1)}, u32[]{:S(2)}, u32[]{:S(2)}) collective-permute-start(f32[64,1,2]{0,2,1:T(2,128)S(1)} %bitcast.204), channel_id=1, source_target_pairs={{0,704},{64,0},{128,64},{192,128},{256,192},{320,256},{384,320},{4... | collective-permute-start | bytes 1544 | tf_op jit(solution)/shard_map/ppermute | solution.py:12
  163.9 0.6 collective-permute-done.10
  164.8 1.9 collective-permute-start.5
  166.7 5.1 %collective-permute-start.4 = (f32[64,1,3,128]{3,1,2,0:T(1,128)S(1)}, f32[64,1,3,128]{3,1,2,0:T(1,128)S(1)}, u32[]{:S(2)}, u32[]{:S(2)}) collective-permute-start(f32[64,1,3,128]{3,1,2,0:T(1,128)S(1)} %get-tuple-element.22), channel_id=1, source_target_pairs={{0,704},{64,0},{128,64},{192,128},{256,192},{320,256},{384,320},{4... | collective-permute-start | bytes 294920 | tf_op jit(solution)/shard_map/ppermute | solution.py:12
  171.9 0.3 collective-permute-done.5
  172.2 1.3 collective-permute-done.4
  173.5 0.3 pad_maximum_fusion.7
  174.0 0.4 copy-done.1
  174.5 22.2 %all-to-all-done.4 = f32[3,64,1,16,128]{4,3,0,2,1:T(8,128)S(1)} async-done(((f32[3,64,1,16,128]{4,3,0,2,1:T(8,128)}), f32[3,64,1,16,128]{4,3,0,2,1:T(8,128)S(1)}, u32[]{:S(2)}, u32[]{:S(2)}) %all-to-all-start.4) | async-done | bytes 1572896 | tf_op jit(solution)/shard_map/all_to_all | solution.py:61
  196.8 1.9 collective-permute-start.9
  198.7 4.8 %collective-permute-start.8 = (f32[64,1,16,128]{3,2,0,1:T(8,128)S(1)}, f32[64,1,16,128]{3,2,0,1:T(8,128)S(1)}, u32[]{:S(2)}, u32[]{:S(2)}) collective-permute-start(f32[64,1,16,128]{3,2,0,1:T(8,128)S(1)} %get-tuple-element.4), channel_id=1, source_target_pairs={{0,704},{64,0},{128,64},{192,128},{256,192},{320,256},{384,320},{4... | collective-permute-start | bytes 1572872 | tf_op jit(solution)/shard_map/ppermute | solution.py:12
  203.5 0.3 broadcast_multiply_fusion
  203.8 1.0 multiply_reduce_fusion
  204.8 0.3 convolution_add_fusion
  205.1 8.2 %collective-permute-done.9 = f32[64,1,16,128]{3,2,0,1:T(8,128)S(1)} collective-permute-done((f32[64,1,16,128]{3,2,0,1:T(8,128)S(1)}, f32[64,1,16,128]{3,2,0,1:T(8,128)S(1)}, u32[]{:S(2)}, u32[]{:S(2)}) %collective-permute-start.9) | collective-permute-done | bytes 524320 | tf_op jit(solution)/shard_map/ppermute | solution.py:12
  213.3 0.9 collective-permute-done.8
  214.3 6.2 %fusion = f32[192,27,16]{1,2,0:T(8,128)S(1)} fusion(f32[192,16,128]{2,1,0:T(8,128)S(1)} %bitcast.175, f32[192,27,128]{2,0,1:T(8,128)S(1)} %bitcast.169), kind=kOutput, calls=%fused_computation.8 | convolution fusion | flops 127401984 | bytes 4558848 | tf_op jit(solution)/shard_map/snb,sfb->snf/dot_general | solution.py:83
  220.6 1.0 copy.380
  221.5 1.2 convolution_divide_fusion
  (89 shorter events, 5.4 us)
Async XLA Ops:
  0.6 21.1 %copy-start = (f32[128,3,128]{2,0,1:T(8,128)S(1)}, f32[128,3,128]{2,0,1:T(8,128)}, u32[]{:S(2)}) copy-start(f32[128,3,128]{2,0,1:T(8,128)} %param.6) | copy-start | bytes 589828
  0.6 21.2 %copy-start.3 = (f32[81,256]{1,0:T(8,128)S(1)}, f32[81,256]{1,0:T(8,128)}, u32[]{:S(2)}) copy-start(f32[81,256]{1,0:T(8,128)} %param.8) | copy-start | bytes 248836
  4.8 24.8 %all-to-all-start = ((f32[3,64,1,4]{3,2,0,1:T(1,128)}), f32[3,64,1,4]{3,2,0,1:T(1,128)S(1)}, u32[]{:S(2)}, u32[]{:S(2)}) async-start(f32[3,64,1,4]{3,2,0,1:T(1,128)} %fusion.23), calls=%async_computation | async-start | bytes 196608 | tf_op jit(solution)/shard_map/all_to_all | solution.py:61
  26.0 2.5 %copy-start.2 = (bf16[128,16,128]{2,1,0:T(8,128)(2,1)S(1)}, bf16[128,16,128]{2,1,0:T(8,128)(2,1)}, u32[]{:S(2)}) copy-start(bf16[128,16,128]{2,1,0:T(8,128)(2,1)} %param.7) | copy-start | bytes 1572868
  29.7 29.0 %all-to-all-start.1 = ((f32[3,64,1,2,3,128]{5,3,4,2,0,1:T(2,128)}), f32[3,64,1,2,3,128]{5,3,4,2,0,1:T(2,128)S(1)}, u32[]{:S(2)}, u32[]{:S(2)}) async-start(f32[3,64,1,2,3,128]{5,3,4,2,0,1:T(2,128)} %fusion.15), calls=%async_computation.1 | async-start | bytes 1179648 | tf_op jit(solution)/shard_map/all_to_all | solution.py:61
  40.1 15.2 %collective-permute-start.1 = (f32[64,1,4]{2,0,1:T(8,128)S(1)}, f32[64,1,4]{2,0,1:T(8,128)S(1)}, u32[]{:S(2)}, u32[]{:S(2)}) collective-permute-start(f32[64,1,4]{2,0,1:T(8,128)S(1)} %bitcast.195), channel_id=1, source_target_pairs={{0,64},{64,128},{128,192},{192,256},{256,320},{320,384},{384,448},... | collective-permute-start | bytes 3080 | tf_op jit(solution)/shard_map/ppermute | solution.py:12
  42.0 13.3 %collective-permute-start = (f32[64,1,4]{2,0,1:T(8,128)S(1)}, f32[64,1,4]{2,0,1:T(8,128)S(1)}, u32[]{:S(2)}, u32[]{:S(2)}) collective-permute-start(f32[64,1,4]{2,0,1:T(8,128)S(1)} %bitcast.194), channel_id=1, source_target_pairs={{0,704},{64,0},{128,64},{192,128},{256,192},{320,256},{384,320},{4... | collective-permute-start | bytes 3080 | tf_op jit(solution)/shard_map/ppermute | solution.py:12
  58.7 47.9 %all-to-all-start.3 = ((f32[3,64,1,16,128]{4,3,0,2,1:T(8,128)}), f32[3,64,1,16,128]{4,3,0,2,1:T(8,128)S(1)}, u32[]{:S(2)}, u32[]{:S(2)}) async-start(f32[3,64,1,16,128]{4,3,0,2,1:T(8,128)} %copy.365), calls=%async_computation.3 | async-start | bytes 3145728 | tf_op jit(solution)/shard_map/all_to_all | solution.py:61
  69.4 14.2 %collective-permute-start.3 = (f32[64,1,2,3,128]{4,2,3,0,1:T(2,128)S(1)}, f32[64,1,2,3,128]{4,2,3,0,1:T(2,128)S(1)}, u32[]{:S(2)}, u32[]{:S(2)}) collective-permute-start(f32[64,1,2,3,128]{4,2,3,0,1:T(2,128)S(1)} %get-tuple-element.11), channel_id=1, source_target_pairs={{0,64},{64,128},{128,192},{192,256},{256,320},{320,384},{384,448},... | collective-permute-start | bytes 589832 | tf_op jit(solution)/shard_map/ppermute | solution.py:12
  71.4 13.2 %collective-permute-start.2 = (f32[64,1,2,3,128]{4,2,3,0,1:T(2,128)S(1)}, f32[64,1,2,3,128]{4,2,3,0,1:T(2,128)S(1)}, u32[]{:S(2)}, u32[]{:S(2)}) collective-permute-start(f32[64,1,2,3,128]{4,2,3,0,1:T(2,128)S(1)} %get-tuple-element.10), channel_id=1, source_target_pairs={{0,704},{64,0},{128,64},{192,128},{256,192},{320,256},{384,320},{4... | collective-permute-start | bytes 589832 | tf_op jit(solution)/shard_map/ppermute | solution.py:12
  106.6 20.9 %all-to-all-start.5 = ((f32[3,64,1,2]{0,3,2,1:T(2,128)}), f32[3,64,1,2]{0,3,2,1:T(2,128)S(1)}, u32[]{:S(2)}, u32[]{:S(2)}) async-start(f32[3,64,1,2]{0,3,2,1:T(2,128)} %select_convert_fusion), calls=%async_computation.5 | async-start | bytes 131072 | tf_op jit(solution)/shard_map/all_to_all | solution.py:61
  113.9 24.3 %collective-permute-start.7 = (f32[64,1,16,128]{3,2,0,1:T(8,128)}, f32[64,1,16,128]{3,2,0,1:T(8,128)S(1)}, u32[]{:S(2)}, u32[]{:S(2)}) collective-permute-start(f32[64,1,16,128]{3,2,0,1:T(8,128)} %get-tuple-element.8), channel_id=1, source_target_pairs={{0,64},{64,128},{128,192},{192,256},{256,320},{320,384},{384,448},... | collective-permute-start | bytes 1572872 | tf_op jit(solution)/shard_map/ppermute | solution.py:12
  115.8 22.4 %collective-permute-start.6 = (f32[64,1,16,128]{3,2,0,1:T(8,128)}, f32[64,1,16,128]{3,2,0,1:T(8,128)}, u32[]{:S(2)}, u32[]{:S(2)}) collective-permute-start(f32[64,1,16,128]{3,2,0,1:T(8,128)} %get-tuple-element.7), channel_id=1, source_target_pairs={{0,704},{64,0},{128,64},{192,128},{256,192},{320,256},{384,320},{4... | collective-permute-start | bytes 1572872 | tf_op jit(solution)/shard_map/ppermute | solution.py:12
  127.6 23.2 %all-to-all-start.2 = ((f32[3,64,1,3,128]{4,2,3,0,1:T(1,128)}), f32[3,64,1,3,128]{4,2,3,0,1:T(1,128)S(1)}, u32[]{:S(2)}, u32[]{:S(2)}) async-start(f32[3,64,1,3,128]{4,2,3,0,1:T(1,128)} %broadcast_select_fusion.1), calls=%async_computation.2 | async-start | bytes 589824 | tf_op jit(solution)/shard_map/all_to_all | solution.py:61
  150.8 45.8 %all-to-all-start.4 = ((f32[3,64,1,16,128]{4,3,0,2,1:T(8,128)}), f32[3,64,1,16,128]{4,3,0,2,1:T(8,128)S(1)}, u32[]{:S(2)}, u32[]{:S(2)}) async-start(f32[3,64,1,16,128]{4,3,0,2,1:T(8,128)} %copy.368), calls=%async_computation.4 | async-start | bytes 3145728 | tf_op jit(solution)/shard_map/all_to_all | solution.py:61
  157.2 6.7 %collective-permute-start.11 = (f32[64,1,2]{0,2,1:T(2,128)S(1)}, f32[64,1,2]{0,2,1:T(2,128)S(1)}, u32[]{:S(2)}, u32[]{:S(2)}) collective-permute-start(f32[64,1,2]{0,2,1:T(2,128)S(1)} %bitcast.203), channel_id=1, source_target_pairs={{0,64},{64,128},{128,192},{192,256},{256,320},{320,384},{384,448},... | collective-permute-start | bytes 1544 | tf_op jit(solution)/shard_map/ppermute | solution.py:12
  159.2 5.3 %collective-permute-start.10 = (f32[64,1,2]{0,2,1:T(2,128)S(1)}, f32[64,1,2]{0,2,1:T(2,128)S(1)}, u32[]{:S(2)}, u32[]{:S(2)}) collective-permute-start(f32[64,1,2]{0,2,1:T(2,128)S(1)} %bitcast.204), channel_id=1, source_target_pairs={{0,704},{64,0},{128,64},{192,128},{256,192},{320,256},{384,320},{4... | collective-permute-start | bytes 1544 | tf_op jit(solution)/shard_map/ppermute | solution.py:12
  164.8 7.4 %collective-permute-start.5 = (f32[64,1,3,128]{3,1,2,0:T(1,128)S(1)}, f32[64,1,3,128]{3,1,2,0:T(1,128)S(1)}, u32[]{:S(2)}, u32[]{:S(2)}) collective-permute-start(f32[64,1,3,128]{3,1,2,0:T(1,128)S(1)} %get-tuple-element.23), channel_id=1, source_target_pairs={{0,64},{64,128},{128,192},{192,256},{256,320},{320,384},{384,448},... | collective-permute-start | bytes 294920 | tf_op jit(solution)/shard_map/ppermute | solution.py:12
  166.7 6.7 %collective-permute-start.4 = (f32[64,1,3,128]{3,1,2,0:T(1,128)S(1)}, f32[64,1,3,128]{3,1,2,0:T(1,128)S(1)}, u32[]{:S(2)}, u32[]{:S(2)}) collective-permute-start(f32[64,1,3,128]{3,1,2,0:T(1,128)S(1)} %get-tuple-element.22), channel_id=1, source_target_pairs={{0,704},{64,0},{128,64},{192,128},{256,192},{320,256},{384,320},{4... | collective-permute-start | bytes 294920 | tf_op jit(solution)/shard_map/ppermute | solution.py:12
  173.8 0.7 copy-start.1
  196.8 16.5 %collective-permute-start.9 = (f32[64,1,16,128]{3,2,0,1:T(8,128)S(1)}, f32[64,1,16,128]{3,2,0,1:T(8,128)S(1)}, u32[]{:S(2)}, u32[]{:S(2)}) collective-permute-start(f32[64,1,16,128]{3,2,0,1:T(8,128)S(1)} %get-tuple-element.5), channel_id=1, source_target_pairs={{0,64},{64,128},{128,192},{192,256},{256,320},{320,384},{384,448},... | collective-permute-start | bytes 1572872 | tf_op jit(solution)/shard_map/ppermute | solution.py:12
  198.7 15.5 %collective-permute-start.8 = (f32[64,1,16,128]{3,2,0,1:T(8,128)S(1)}, f32[64,1,16,128]{3,2,0,1:T(8,128)S(1)}, u32[]{:S(2)}, u32[]{:S(2)}) collective-permute-start(f32[64,1,16,128]{3,2,0,1:T(8,128)S(1)} %get-tuple-element.4), channel_id=1, source_target_pairs={{0,704},{64,0},{128,64},{192,128},{256,192},{320,256},{384,320},{4... | collective-permute-start | bytes 1572872 | tf_op jit(solution)/shard_map/ppermute | solution.py:12
where the time goes:
time: 224 us; the launch traced here: 223 us
  starting transfers between devices  112 us (50%)
  waiting for transfers between devices  64.8 us (29%)
  local copies, waits for them, and re-layouts  16.3 us (7%)
  matrix products  14.4 us (6%)
  other arithmetic  13.2 us (6%)
    ppermute x12, starting transfers between devices, passed_along(): return lax.ppermute(x, axis, [(i, (i + by) % size) for i in range(size)])  56.2 us
    all_to_all x6, starting transfers between devices, migrate(): lax.all_to_all(shaped, 'rad', split_axis=1, concat_axis=1, tiled=True)  55.8 us
    all_to_all x6, waiting for transfers between devices, migrate(): lax.all_to_all(shaped, 'rad', split_axis=1, concat_axis=1, tiled=True)  50.6 us
    ppermute x12, waiting for transfers between devices, passed_along(): return lax.ppermute(x, axis, [(i, (i + by) % size) for i in range(size)])  14.2 us
    dot_general x2, matrix products, speed(): jnp.einsum('scn,snb->scb', coefficients, basis(points), precision=exact)  6.7 us
    dot_general x1, matrix products, block_sums(): moments = jnp.einsum('snb,sfb->snf', shapes, carried, precision=exact)  6.25 us
    gather x7, local copies, waits for them, and re-layouts, arrange(): picked = jnp.take(member, source, axis=0)  5.72 us
  transfers between devices with their start and end apart: 18, of which 12 were waited for; matrix products, arithmetic and copies ran while one was open for 14% of the time, Pallas kernels for 0%

commit v1 on v0

v1 whole, which is shorter than its diff:
```python
import functools

import jax
import jax.numpy as jnp
from jax import lax
from jax.experimental import pallas as pl
from jax.experimental.pallas import tpu as pltpu
from jax.sharding import PartitionSpec as P

time_step = 0.4
exact = lax.Precision.HIGHEST
MESH = pl.DeviceIdType.MESH
LANES = 128
NX, NY, NC = 4, 8, 2


def lagrange(coord):
    first_node = 2.0 * (coord - 0.5) * (coord - 1.0)
    middle_node = -4.0 * coord * (coord - 1.0)
    last_node = 2.0 * coord * (coord - 0.5)
    return jnp.stack([first_node, middle_node, last_node], axis=0)


def basis(points):
    along_x = lagrange(points[:, 0, :])
    along_y = lagrange(points[:, 1, :])
    along_z = lagrange(points[:, 2, :])
    table = along_x[:, None, None] * along_y[None, :, None] * along_z[None, None, :]
    return jnp.moveaxis(table.reshape(27, points.shape[0], points.shape[2]), 0, 1)


def speed(coefficients, points):
    return jnp.einsum("scn,snb->scb", coefficients.reshape(-1, 3, 27), basis(points), precision=exact)


def exchange_kernel(lat_count, rad_count, rows, back, x_ref, o_ref, lsem, ssem, rsem):
    lat = lax.axis_index("lat")
    rad = lax.axis_index("rad")
    places = 3 * rad_count
    x0, y0, c0 = rad // (NY * NC), lax.rem(rad // NC, NY), lax.rem(rad, NC)

    def partner(i):
        m = NY - 1 - lax.rem(i, NY)
        h = (m + 1) // 2
        dy = lax.rem(jnp.where(lax.rem(m, 2) == 1, h, NY - h), NY)
        j = i // NY
        dc = lax.rem(j, NC)
        dx = lax.rem(j // NC + lax.rem(m, NX), NX)
        return (lax.rem(x0 + dx, NX) * NY + lax.rem(y0 + dy, NY)) * NC + lax.rem(c0 + dc, NC)

    def over_partners(act):
        def step(i, carry):
            q = partner(i)
            for k in range(3):
                shift = (1 - k) if back else (k - 1)
                target = (lax.rem(lat + shift + lat_count, lat_count), q)
                if k == 1:
                    @pl.when(q != rad)
                    def _():
                        act(k, q, target)
                else:
                    act(k, q, target)
            return carry

        lax.fori_loop(0, rad_count, step, 0)

    barrier = pltpu.get_barrier_semaphore()
    over_partners(
        lambda k, q, target: pl.semaphore_signal(barrier, inc=1, device_id=target, device_id_type=MESH)
    )
    pl.semaphore_wait(barrier, places - 1)

    def send(k, q, target):
        pltpu.make_async_remote_copy(
            src_ref=x_ref.at[k * rad_count + q, pl.ds(0, rows)],
            dst_ref=o_ref.at[k * rad_count + rad, pl.ds(0, rows)],
            send_sem=ssem, recv_sem=rsem, device_id=target, device_id_type=MESH,
        ).start()

    over_partners(send)
    mine = rad_count + rad
    local = pltpu.make_async_copy(x_ref.at[mine, pl.ds(0, rows)], o_ref.at[mine, pl.ds(0, rows)], lsem)
    local.start()
    local.wait()
    span = o_ref.at[pl.ds(0, places - 1), pl.ds(0, rows)]
    pltpu.make_async_copy(span, span, rsem).wait()
    pltpu.make_async_copy(span, span, ssem).wait()


def exchange(x, rows, back, number):
    lat_count, rad_count = lax.axis_size("lat"), lax.axis_size("rad")
    return pl.pallas_call(
        functools.partial(exchange_kernel, lat_count, rad_count, rows, back),
        out_shape=jax.ShapeDtypeStruct(x.shape, x.dtype),
        in_specs=[pl.BlockSpec(memory_space=pltpu.VMEM)],
        out_specs=pl.BlockSpec(memory_space=pltpu.VMEM),
        scratch_shapes=[pltpu.SemaphoreType.DMA, pltpu.SemaphoreType.DMA, pltpu.SemaphoreType.DMA],
        compiler_params=pltpu.CompilerParams(collective_id=number, has_side_effects=True),
        name=f"exchange{number}",
    )(x)


def place_rows(target, valid, number):
    matches = (target[:, None] == jnp.arange(number, dtype=jnp.int32)[None, :]) & valid[:, None]
    present = jnp.any(matches, axis=0)
    source = jnp.sum(jnp.where(matches, jnp.arange(target.shape[0], dtype=jnp.int32)[:, None], 0), axis=0)
    return source, present


def arrange(member, source, present):
    picked = jnp.take(member, source, axis=0)
    return jnp.where(present.reshape((-1,) + (1,) * (member.ndim - 1)), picked, 0.0)


def widen(flat, rows):
    flat = jnp.pad(flat, ((0, 0), (0, rows * LANES - flat.shape[1])))
    return flat.reshape(-1, rows, LANES)


def per_device(positions, fields, velocity, counts, elements, routes):
    rad_count = lax.axis_size("rad")
    places = 3 * rad_count
    blocks = positions.shape[0]
    owned = velocity.shape[1]
    table = velocity.T
    home_valid = jnp.arange(blocks, dtype=jnp.int32) < counts[0]
    source, present = place_rows(routes[0], home_valid, places)
    labels = jnp.stack(
        [home_valid.astype(jnp.int32), elements[1], routes[1], elements[2]], axis=1
    ).astype(jnp.float32)
    asked = exchange(widen(arrange(labels, source, present), 8), 1, False, 0)[:, 0, :4].astype(jnp.int32)
    first_speed = speed(jnp.take(table, elements[0], axis=0), positions)
    midway = positions + 0.5 * time_step * first_speed
    mid_valid = asked[:, 0] > 0
    answered = exchange(widen(jnp.take(table, asked[:, 1], axis=0), 8), 1, True, 1)[:, 0, :81]
    landed = positions + time_step * speed(jnp.take(answered, routes[0], axis=0), midway)
    shapes = basis(landed)
    moments = jnp.einsum("snb,sfb->snf", shapes, fields.astype(jnp.float32), precision=exact)
    weights = jnp.sum(shapes * shapes, axis=2)
    cargo = jnp.concatenate([landed.reshape(blocks, -1), moments.reshape(blocks, -1), weights], axis=1)
    cargo = exchange(arrange(widen(cargo, 8), source, present), 7, False, 2)
    source, present = place_rows(asked[:, 2], mid_valid, places)
    cargo = cargo.at[:, 6, LANES - 1].set((asked[:, 3] + 1).astype(jnp.float32))
    cargo = exchange(arrange(cargo, source, present), 7, False, 3)
    tags = cargo[:, 6, LANES - 1].astype(jnp.int32) - 1
    cargo = cargo.reshape(places, -1)
    moved = cargo[:, : 3 * LANES].reshape(places, 3, LANES)
    hits = (tags[:, None] == jnp.arange(owned, dtype=jnp.int32)[None, :]).astype(jnp.float32)
    start = 3 * LANES
    totals = jnp.einsum("sm,se->me", cargo[:, start : start + 432], hits, precision=exact)
    summed = jnp.einsum("sn,se->ne", cargo[:, start + 432 : start + 459], hits, precision=exact)
    projected = totals.reshape(27, 16, owned) / (1.0 + summed[:, None, :])
    return moved, projected


def solution(mesh):
    in_specs = (
        P(("lat", "rad"), None, None),
        P(("lat", "rad"), None, None),
        P(None, ("lat", "rad")),
        P(("lat", "rad")),
        P(None, ("lat", "rad")),
        P(None, ("lat", "rad")),
    )
    out_specs = (P(("lat", "rad"), None, None), P(None, None, ("lat", "rad")))
    return jax.shard_map(
        per_device, mesh=mesh, in_specs=in_specs, out_specs=out_specs, check_vma=False
    )
```

time: 224 us -> 181 us (0.81)
  Pallas kernels: 0 us -> 124 us
  starting transfers between devices: 112 us -> 0 us
  waiting for transfers between devices: 64.8 us -> 0 us
  local copies, waits for them, and re-layouts: 16.3 us -> 33.1 us
  matrix products: 14.4 us -> 8.88 us
    pallas_call x0 -> x4, Pallas kernels: none -> 124 us  [exchange(): pl.pallas_call(functools.partial(exchange_kernel, lat_count, rad_count, r...]
    ppermute x12 -> x0, starting transfers between devices: 56.2 us -> none  [passed_along(): return lax.ppermute(x, axis, [(i, (i + by) % size) for i in range(size)])]
    all_to_all x6 -> x0, starting transfers between devices: 55.8 us -> none  [migrate(): lax.all_to_all(shaped, 'rad', split_axis=1, concat_axis=1, tiled=True)]
    all_to_all x6 -> x0, waiting for transfers between devices: 50.6 us -> none  [migrate(): lax.all_to_all(shaped, 'rad', split_axis=1, concat_axis=1, tiled=True)]
    scatter x0 -> x1, local copies, waits for them, and re-layouts: none -> 17.9 us  [per_device(): cargo = cargo.at[:, 6, LANES - 1].set((asked[:, 3] + 1).astype(jnp.float32))]
    ppermute x12 -> x0, waiting for transfers between devices: 14.2 us -> none  [passed_along(): return lax.ppermute(x, axis, [(i, (i + by) % size) for i in range(size)])]
    dot_general x5, matrix products: 14.4 us -> 8.88 us  [the longest x2 5.39 us: speed(): jnp.einsum('scn,snb->scb', coefficients.reshape(-1, 3, 27), basis(points)...]
    sub x0 -> x1, other arithmetic: none -> 4.91 us  [per_device(): tags = cargo[:, 6, LANES - 1].astype(jnp.int32) - 1]
  transfers between devices with their start and end apart: 18 -> 0, of which waited for: 12 -> 0; matrix products, arithmetic and copies ran while one was open for 14% -> 0% of each run, Pallas kernels for 0% -> 0%
where the time goes in v1:
time: 181 us
  Pallas kernels  124 us (69%)
  local copies, waits for them, and re-layouts  33.1 us (18%)
  other arithmetic  13.5 us (7%)
  matrix products  8.88 us (5%)
    pallas_call x4, Pallas kernels, exchange(): pl.pallas_call(functools.partial(exchange_kernel, lat_count, rad_count, r...  124 us
    scatter x1, local copies, waits for them, and re-layouts, per_device(): cargo = cargo.at[:, 6, LANES - 1].set((asked[:, 3] + 1).astype(jnp.float32))  17.9 us
    dot_general x2, matrix products, speed(): jnp.einsum('scn,snb->scb', coefficients.reshape(-1, 3, 27), basis(points)...  5.39 us
    unnamed x15, local copies, waits for them, and re-layouts  5.28 us
    sub x1, other arithmetic, per_device(): tags = cargo[:, 6, LANES - 1].astype(jnp.int32) - 1  4.91 us

profile of v1, /device:TPU:1, one launch (start us, length us, event | category | flops | bytes accessed | tf_op | source)
XLA Modules:
  0.0 180.7 jit_solution(9378252674498536523)
XLA Ops:
  0.6 0.0 copy-start
  0.6 1.0 copy.149
  1.7 0.8 slice_bitcast_fusion.3
  2.5 0.8 slice_bitcast_fusion.4
  3.9 0.1 copy.148
  4.0 0.1 select_reduce_fusion.1
  4.1 0.1 copy.145
  4.3 0.1 fusion.12
  4.4 0.7 gather_fusion
  5.1 0.1 fusion.19
  5.2 0.1 select_select_fusion.2
  5.4 0.1 pad_bitcast_fusion.1
  5.4 1.0 copy.168
  6.5 32.5 %exchange0.1 = f32[192,8,128]{2,1,0:T(8,128)} custom-call(f32[192,8,128]{2,1,0:T(8,128)} %bitcast.131), custom_call_target="tpu_custom_call" | custom-call | tf_op jit(solution)/shard_map/exchange0/pallas_call | solution.py:92
  39.0 1.2 slice_convert_fusion
  40.2 0.3 slice_reduce_fusion
  40.5 0.7 gather_fusion.1
  41.2 0.2 fusion.20
  41.4 0.1 broadcast_select_fusion
  41.5 0.1 pad_bitcast_fusion
  41.6 0.0 copy-start.2
  41.6 1.0 copy.169
  42.6 20.2 %exchange1.1 = f32[192,8,128]{2,1,0:T(8,128)} custom-call(f32[192,8,128]{2,1,0:T(8,128)} %bitcast.132), custom_call_target="tpu_custom_call" | custom-call | tf_op jit(solution)/shard_map/exchange1/pallas_call | solution.py:92
  62.8 1.2 slice.103
  64.0 0.0 copy-done.2
  64.1 0.6 gather_fusion.2
  64.7 0.1 copy.150
  64.8 0.2 copy.155
  65.0 0.0 copy-done.3
  65.1 0.6 gather_fusion.3
  65.7 0.1 copy.151
  65.8 0.2 copy.152
  66.0 0.0 copy-done.1
  66.0 0.1 multiply_bitcast_fusion.26
  66.2 0.2 broadcast_multiply_fusion.2
  66.4 2.7 %fusion.4 = f32[128,3,128]{2,1,0:T(4,128)S(1)} fusion(f32[128,3,27]{2,1,0:T(4,128)S(1)} %copy.152, f32[128,27,128]{2,0,1:T(8,128)S(1)} %bitcast.122), kind=kOutput, calls=%fused_computation.10 | convolution fusion | flops 15925248 | bytes 2007552 | tf_op jit(solution)/shard_map/scn,snb->scb/dot_general | solution.py:33
  69.1 0.1 multiply_bitcast_fusion.17
  69.3 0.2 broadcast_multiply_fusion.1
  69.5 2.7 %fusion.2 = f32[128,3,128]{2,1,0:T(4,128)S(1)} fusion(f32[128,3,27]{2,1,0:T(4,128)S(1)} %copy.155, f32[128,27,128]{2,0,1:T(8,128)S(1)} %bitcast.123), kind=kOutput, calls=%fused_computation.8 | convolution fusion | flops 15925248 | bytes 2007552 | tf_op jit(solution)/shard_map/scn,snb->scb/dot_general | solution.py:33
  72.2 0.1 multiply_bitcast_fusion.8
  72.4 0.2 broadcast_multiply_fusion
  72.7 0.5 multiply_reduce_fusion
  73.2 0.0 copy-done
  73.2 2.5 %fusion = f32[128,27,16]{1,2,0:T(8,128)S(1)} fusion(bf16[128,16,128]{2,1,0:T(8,128)(2,1)S(1)} %copy-done, f32[128,27,128]{2,0,1:T(8,128)S(1)} %bitcast.119), kind=kOutput, calls=%fused_computation.6 | convolution fusion | flops 84934656 | bytes 2514944 | tf_op jit(solution)/shard_map/snb,sfb->snf/dot_general | solution.py:138
  75.8 0.5 copy.160
  76.3 0.1 copy.158
  76.4 0.2 copy.166
  76.7 0.9 gather_fusion.4
  77.6 1.7 select_select_fusion.1.x_ref
  79.3 36.0 %exchange2.1 = f32[192,8,128]{2,1,0:T(8,128)} custom-call(f32[192,8,128]{2,1,0:T(8,128)} %select_select_fusion.1.x_ref), custom_call_target="tpu_custom_call" | custom-call | tf_op jit(solution)/shard_map/exchange2/pallas_call | solution.py:92
  115.2 17.9 %scatter.4 = f32[192,8,128]{2,1,0:T(8,128)} dynamic-update-slice(f32[192,8,128]{2,1,0:T(8,128)} %exchange2.1, f32[192,1,1]{2,1,0:T(1,128)S(1)} %bitcast.137, s32[]{:T(128)} %constant.136.clone.1, s32[]{:T(128)} %constant.152.clone.1, s32[]{:T(128)} %constant.138.clone.1) | dynamic-update-slice | bytes 1540 | tf_op jit(solution)/shard_map/scatter | solution.py:143
  133.2 0.1 select_reduce_fusion
  133.3 0.1 copy.162
  133.4 0.1 fusion.13
  133.6 1.8 %gather_fusion.5 = f32[192,8,128]{2,1,0:T(8,128)S(1)} fusion(f32[192,8,128]{2,1,0:T(8,128)} %scatter.4, s32[1024]{0:T(1024)S(1)} %pad_clamp_fusion), kind=kCustom, calls=%fused_computation.5 | custom fusion | bytes 1573632 | tf_op jit(solution)/shard_map/jit(_take)/gather | solution.py:111
  135.4 0.1 fusion.11
  135.6 1.6 select_select_fusion.x_ref
  137.2 34.8 %exchange3.1 = f32[192,8,128]{2,1,0:T(8,128)} custom-call(f32[192,8,128]{2,1,0:T(8,128)} %select_select_fusion.x_ref), custom_call_target="tpu_custom_call" | custom-call | tf_op jit(solution)/shard_map/exchange3/pallas_call | solution.py:92
  172.1 1.3 copy.185
  173.3 0.7 copy_bitcast_fusion.1
  174.1 4.9 %add_reduce_fusion = s32[192]{0:T(256)S(1)} fusion(f32[192,8,128]{2,1,0:T(8,128)} %exchange3.1), kind=kLoop, calls=%fused_computation.63 | loop fusion | flops 384 | bytes 1536 | tf_op jit(solution)/shard_map/sub | solution.py:145
  179.0 0.6 fusion.6
  179.6 0.3 convolution_add_fusion
  179.9 0.8 broadcast_divide_fusion
  (34 shorter events, 0.5 us)
Async XLA Ops:
  0.6 72.6 %copy-start = (bf16[128,16,128]{2,1,0:T(8,128)(2,1)S(1)}, bf16[128,16,128]{2,1,0:T(8,128)(2,1)}, u32[]{:S(2)}) copy-start(bf16[128,16,128]{2,1,0:T(8,128)(2,1)} %param.9) | copy-start | bytes 1572868
  41.6 22.5 %copy-start.2 = (s32[2,128]{1,0:T(2,128)S(1)}, s32[2,128]{1,0:T(2,128)}, u32[]{:S(2)}) copy-start(s32[2,128]{1,0:T(2,128)} %param.13) | copy-start | bytes 3076
  42.6 22.4 %copy-start.3 = (s32[3,128]{1,0:T(4,128)S(1)}, s32[3,128]{1,0:T(4,128)}, u32[]{:S(2)}) copy-start(s32[3,128]{1,0:T(4,128)} %param.12) | copy-start | bytes 4612
  42.6 23.4 %copy-start.1 = (f32[128,3,128]{2,0,1:T(8,128)S(1)}, f32[128,3,128]{2,0,1:T(8,128)}, u32[]{:S(2)}) copy-start(f32[128,3,128]{2,0,1:T(8,128)} %param.8) | copy-start | bytes 589828

commit v2 on v0

v2 whole, which is shorter than its diff:
```python
import functools

import jax
import jax.numpy as jnp
from jax import lax
from jax.experimental import pallas as pl
from jax.experimental.pallas import tpu as pltpu
from jax.sharding import PartitionSpec as P

time_step = 0.4
exact = lax.Precision.HIGHEST
MESH = pl.DeviceIdType.MESH
LANES = 128
GROUP = 8
NX, NY, NC = 4, 8, 2
NODES = 27
COLUMNS = 3 * NODES
ASKED, ROUTE, HOME = 81, 82, 83
WEIGHTS, TAG = 48, 127
CHUNKS = ((3, 0), (1, 2))
NT = (((1,), (1,)), ((), ()))
TN = (((0,), (0,)), ((), ()))


def product(a, b, dims=(((1,), (0,)), ((), ()))):
    return lax.dot_general(a, b, dims, precision=exact, preferred_element_type=jnp.float32)


def iota(shape, axis):
    return lax.broadcasted_iota(jnp.int32, shape, axis)


def onehot(mask):
    return jnp.where(mask, 1.0, 0.0)


def lagrange(s):
    return 2.0 * (s - 0.5) * (s - 1.0), -4.0 * s * (s - 1.0), 2.0 * s * (s - 0.5)


def speed(coefficients, points):
    along = [lagrange(p) for p in points]
    result = []
    for c in range(3):
        total = None
        for i in range(3):
            plane = None
            for j in range(3):
                line = None
                for k in range(3):
                    n = c * NODES + 9 * i + 3 * j + k
                    term = coefficients[:, n : n + 1] * along[2][k]
                    line = term if line is None else line + term
                line = line * along[1][j]
                plane = line if plane is None else plane + line
            plane = plane * along[0][i]
            total = plane if total is None else total + plane
        result.append(total)
    return result


def basis(points):
    along = [lagrange(p) for p in points]
    shapes = []
    for i in range(3):
        for j in range(3):
            both = along[0][i] * along[1][j]
            for k in range(3):
                shapes.append(both * along[2][k])
    return shapes


def halves(x):
    high = x.astype(jnp.bfloat16)
    return jnp.concatenate([high, (x - high.astype(jnp.float32)).astype(jnp.bfloat16)], axis=0)


def kernel(
    lat_count, rad_count, blocks, owned,
    counts, elements, routes, positions, fields, velocity,
    moved, totals,
    raw, pos, fld, vel, grid, coef, mid, mom, lnd,
    req_s, req_r, rep_s, rep_r, pos_s, pos_r, lnd_s, one_s, one_r, two_s, two_r,
    load_sems, self_sem, send_sems, recv_sems,
):
    lat = lax.axis_index("lat")
    rad = lax.axis_index("rad")
    places = 3 * rad_count
    mine = rad_count + rad
    x0, y0, c0 = rad // (NY * NC), lax.rem(rad // NC, NY), lax.rem(rad, NC)

    def lat_at(shift):
        return lax.rem(lat + shift + lat_count, lat_count)

    def over_partners(act, back=False):
        lats = [lat_at((1 - k) if back else (k - 1)) for k in range(3)]

        def step(j, carry):
            for m in reversed(range(NY)):
                dy = ((m + 1) // 2 if m % 2 else NY - (m + 1) // 2) % NY
                x = lax.rem(x0 + j // NC + m % NX, NX)
                y = lax.rem(y0 + dy, NY)
                q = (x * NY + y) * NC + lax.rem(c0 + j, NC)
                for k in range(3):
                    if k == 1 and m == 0:
                        @pl.when(j != 0)
                        def _():
                            act(k, q, (lats[k], q))
                    else:
                        act(k, q, (lats[k], q))
            return carry

        lax.fori_loop(0, NX * NC, step, 0)

    def send(source, target, number, rows, back=False):
        local = pltpu.make_async_copy(
            source.at[mine, pl.ds(0, rows)], target.at[mine, pl.ds(0, rows)], self_sem
        )
        local.start()

        def act(k, q, device):
            pltpu.make_async_remote_copy(
                src_ref=source.at[k * rad_count + q, pl.ds(0, rows)],
                dst_ref=target.at[k * rad_count + rad, pl.ds(0, rows)],
                send_sem=send_sems.at[number], recv_sem=recv_sems.at[number],
                device_id=device, device_id_type=MESH,
            ).start()

        over_partners(act, back)
        local.wait()

    def settle(buffer, sems, number, rows):
        span = buffer.at[pl.ds(0, places - 1), pl.ds(0, rows)]
        pltpu.make_async_copy(span, span, sems.at[number]).wait()

    loads = [
        pltpu.make_async_copy(velocity, raw, load_sems.at[0]),
        pltpu.make_async_copy(positions, pos, load_sems.at[1]),
        pltpu.make_async_copy(fields, fld, load_sems.at[2]),
    ]
    for load in loads:
        load.start()
    barrier = pltpu.get_barrier_semaphore()
    over_partners(
        lambda k, q, device: pl.semaphore_signal(barrier, inc=1, device_id=device, device_id_type=MESH)
    )

    live = iota((1, blocks), 1) < counts[0]
    element = elements[...]
    route = routes[...]
    first_route = jnp.where(live, route[0:1], -1)
    to_place = onehot(iota((places, blocks), 0) == first_route)
    loads[0].wait()
    vel[pl.ds(80, 48), :] = jnp.zeros((48, owned), jnp.float32)
    vel[pl.ds(0, COLUMNS), :] = raw[...]
    start_hits = onehot(iota((owned, blocks), 0) == element[0:1])
    row = iota((LANES, blocks), 0)
    labels = jnp.where(
        row == ASKED, element[1:2] + 1, jnp.where(row == ROUTE, route[1:2], jnp.where(row == HOME, first_route, 0))
    )
    columns = product(vel[...], start_hits) + labels.astype(jnp.float32)
    req_s[:, 0, :] = product(to_place, columns, NT)
    pl.semaphore_wait(barrier, places - 1)
    send(req_s, req_r, 0, 1)

    grid[...] = columns.T
    loads[1].wait()
    for c in range(3):
        pos_s[:, c, :] = product(to_place, pos[:, c, :])

    def first_step(g, carry):
        rows = pl.ds(pl.multiple_of(g * GROUP, GROUP), GROUP)
        points = [pos[rows, c, :] for c in range(3)]
        for c, u in enumerate(speed(grid[rows, :], points)):
            mid[c, rows, :] = points[c] + 0.5 * time_step * u
        return carry

    lax.fori_loop(0, blocks // GROUP, first_step, 0)

    settle(req_r, recv_sems, 0, 1)
    asked = req_r[:, 0, :]
    middle_hits = onehot(iota((places, owned), 1) == asked[:, ASKED : ASKED + 1].astype(jnp.int32) - 1)
    rep_s[:, 0, :] = product(middle_hits, vel[...], NT)
    send(rep_s, rep_r, 1, 1, back=True)
    send(pos_s, pos_r, 2, 3)
    pick = onehot(iota((GROUP, LANES), 1) == iota((GROUP, LANES), 0) + ASKED)
    turned = product(pick, asked, NT)
    second_route = jnp.where(turned[0:1] > 0.5, turned[1:2].astype(jnp.int32), -1)
    to_final = onehot(iota((places, places), 0) == second_route)
    loads[2].wait()

    settle(rep_r, recv_sems, 1, 1)
    from_place = onehot(iota((blocks, places), 1) == grid[:, HOME : HOME + 1].astype(jnp.int32))
    coef[...] = product(from_place, rep_r[:, 0, :])
    lane = iota((GROUP, LANES), 1)
    own = lane // 16 == iota((GROUP, LANES), 0)
    every = jnp.ones((LANES, LANES), jnp.bfloat16)

    def second_step(g, carry):
        rows = pl.ds(pl.multiple_of(g * GROUP, GROUP), GROUP)
        points = [mid[c, rows, :] for c in range(3)]
        moves = speed(coef[rows, :], points)
        shapes = jnp.concatenate(basis([pos[rows, c, :] + time_step * moves[c] for c in range(3)]), axis=0)
        count = NODES * GROUP
        block_fields = fld[rows].reshape(GROUP * 16, LANES)
        crossed = lax.dot_general(halves(shapes), block_fields, NT, preferred_element_type=jnp.float32)
        crossed = crossed[:count] + crossed[count:]
        squares = lax.dot_general(
            halves(shapes * shapes), every, NT, preferred_element_type=jnp.float32
        )
        squares = squares[:count] + squares[count:]
        for r in range(4):
            total = jnp.zeros((GROUP, LANES), jnp.float32)
            for n in range(8 * r, min(8 * r + 8, NODES)):
                part = jnp.where(own, crossed[n * GROUP : (n + 1) * GROUP], 0.0)
                total += pltpu.roll(part, 16 * (n - 8 * r), 1) if n % 8 else part
            for bit in range(3):
                shift = 16 << bit
                odd = (iota((GROUP, LANES), 0) // (1 << bit)) % 2 == 1
                total = jnp.where(odd, pltpu.roll(total, LANES - shift, 1), total)
            if r == 3:
                for n in range(NODES):
                    total = jnp.where(lane == WEIGHTS + n, squares[n * GROUP : (n + 1) * GROUP], total)
            mom[r, rows, :] = total
        return carry

    lax.fori_loop(0, blocks // GROUP, second_step, 0)
    tags = product(
        onehot(iota((LANES, blocks), 0) == iota((LANES, blocks), 1)),
        jnp.where(iota((LANES, blocks), 0) == TAG, element[2:3] + 1, 0).astype(jnp.float32), NT,
    )
    mom[3] = mom[3] + jnp.where(iota((blocks, LANES), 1) == TAG, tags, 0.0)
    for number, chunk in enumerate(CHUNKS):
        for place, r in enumerate(chunk):
            one_s[number, :, place, :] = product(to_place, mom[r])
        send(one_s.at[number], one_r.at[number], 3 + number, len(chunk))

    settle(pos_r, recv_sems, 2, 3)

    def middle_step(g, carry):
        rows = pl.ds(pl.multiple_of(g * GROUP, GROUP), GROUP)
        points = [pos_r[rows, c, :] for c in range(3)]
        first = speed(req_r[rows, 0, :], points)
        halfway = [points[c] + 0.5 * time_step * first[c] for c in range(3)]
        second = speed(rep_s[rows, 0, :], halfway)
        for c in range(3):
            lnd[c, rows, :] = points[c] + time_step * second[c]
        return carry

    lax.fori_loop(0, places // GROUP, middle_step, 0)
    for c in range(3):
        lnd_s[:, c, :] = product(to_final, lnd[c])
    send(lnd_s, moved, 7, 3)

    for number, chunk in enumerate(CHUNKS):
        settle(one_r.at[number], recv_sems, 3 + number, len(chunk))
        for place in range(len(chunk)):
            two_s[number, :, place, :] = product(to_final, one_r[number, :, place, :])
        send(two_s.at[number], two_r.at[number], 5 + number, len(chunk))

    hits = None
    for number, chunk in enumerate(CHUNKS):
        settle(two_r.at[number], recv_sems, 5 + number, len(chunk))
        for place, r in enumerate(chunk):
            arrived = two_r[number, :, place, :]
            if hits is None:
                hits = onehot(iota((places, owned), 1) == arrived[:, TAG : TAG + 1].astype(jnp.int32) - 1)
            totals[pl.ds(r * LANES, LANES), :] = product(arrived, hits, TN)
    settle(moved, recv_sems, 7, 3)
    for number, (buffer, rows) in enumerate(
        [(req_r, 1), (rep_r, 1), (pos_r, 3), (one_r.at[0], 2), (one_r.at[1], 2), (two_r.at[0], 2), (two_r.at[1], 2), (moved, 3)]
    ):
        settle(buffer, send_sems, number, rows)


def per_device(positions, fields, velocity, counts, elements, routes):
    lat_count, rad_count = lax.axis_size("lat"), lax.axis_size("rad")
    places = 3 * rad_count
    blocks = positions.shape[0]
    owned = velocity.shape[1]
    buffer = pltpu.VMEM((places, 8, LANES), jnp.float32)
    pair = pltpu.VMEM((2, places, 8, LANES), jnp.float32)
    vmem = pl.BlockSpec(memory_space=pltpu.VMEM)
    anywhere = pl.BlockSpec(memory_space=pl.ANY)
    moved, totals = pl.pallas_call(
        functools.partial(kernel, lat_count, rad_count, blocks, owned),
        out_shape=[
            jax.ShapeDtypeStruct((places, 8, LANES), jnp.float32),
            jax.ShapeDtypeStruct((4 * LANES, owned), jnp.float32),
        ],
        in_specs=[pl.BlockSpec(memory_space=pltpu.SMEM), vmem, vmem, anywhere, anywhere, anywhere],
        out_specs=[vmem, vmem],
        scratch_shapes=[
            pltpu.VMEM(velocity.shape, jnp.float32),
            pltpu.VMEM(positions.shape, jnp.float32),
            pltpu.VMEM(fields.shape, fields.dtype),
            pltpu.VMEM((LANES, owned), jnp.float32),
            pltpu.VMEM((blocks, LANES), jnp.float32),
            pltpu.VMEM((blocks, LANES), jnp.float32),
            pltpu.VMEM((3, blocks, LANES), jnp.float32),
            pltpu.VMEM((4, blocks, LANES), jnp.float32),
            pltpu.VMEM((3, places, LANES), jnp.float32),
            buffer, buffer, buffer, buffer, buffer, buffer, buffer, pair, pair, pair, pair,
            pltpu.SemaphoreType.DMA((3,)),
            pltpu.SemaphoreType.DMA,
            pltpu.SemaphoreType.DMA((8,)),
            pltpu.SemaphoreType.DMA((8,)),
        ],
        compiler_params=pltpu.CompilerParams(collective_id=0, has_side_effects=True),
        name="advect",
    )(counts, elements, routes, positions, fields, velocity)
    weights = totals[3 * LANES + WEIGHTS : 3 * LANES + WEIGHTS + NODES]
    projected = totals[: NODES * 16].reshape(NODES, 16, owned) / (1.0 + weights[:, None, :])
    return moved[:, :3], projected


def solution(mesh):
    in_specs = (
        P(("lat", "rad"), None, None),
        P(("lat", "rad"), None, None),
        P(None, ("lat", "rad")),
        P(("lat", "rad")),
        P(None, ("lat", "rad")),
        P(None, ("lat", "rad")),
    )
    out_specs = (P(("lat", "rad"), None, None), P(None, None, ("lat", "rad")))
    return jax.shard_map(
        per_device, mesh=mesh, in_specs=in_specs, out_specs=out_specs, check_vma=False
    )
```

time: 224 us -> 128 us (0.57)
  Pallas kernels: 0 us -> 121 us
  starting transfers between devices: 112 us -> 0 us
  waiting for transfers between devices: 64.8 us -> 0 us
  matrix products: 14.4 us -> 0 us
  other arithmetic: 13.2 us -> 0.81 us
  local copies, waits for them, and re-layouts: 16.3 us -> 4.12 us
    pallas_call x0 -> x1, Pallas kernels: none -> 121 us  [per_device(): pl.pallas_call(functools.partial(kernel, lat_count, rad_count, blocks, ow...]
    ppermute x12 -> x0, starting transfers between devices: 56.2 us -> none  [passed_along(): return lax.ppermute(x, axis, [(i, (i + by) % size) for i in range(size)])]
    all_to_all x6 -> x0, starting transfers between devices: 55.8 us -> none  [migrate(): lax.all_to_all(shaped, 'rad', split_axis=1, concat_axis=1, tiled=True)]
    all_to_all x6 -> x0, waiting for transfers between devices: 50.6 us -> none  [migrate(): lax.all_to_all(shaped, 'rad', split_axis=1, concat_axis=1, tiled=True)]
    dot_general x5 -> x0, matrix products: 14.4 us -> none  [the longest x2 6.7 us: speed(): jnp.einsum('scn,snb->scb', coefficients, basis(points), precision=exact)]
    ppermute x12 -> x0, waiting for transfers between devices: 14.2 us -> none  [passed_along(): return lax.ppermute(x, axis, [(i, (i + by) % size) for i in range(size)])]
    gather x9 -> x0, local copies, waits for them, and re-layouts: 7.06 us -> none  [the longest x7 5.72 us: arrange(): picked = jnp.take(member, source, axis=0)]
    select_n x9 -> x0, other arithmetic: 4.66 us -> none  [the longest x4 3.79 us: arrange(): jnp.where(present.reshape(layout), picked, jnp.zeros_like(picked))]
  transfers between devices with their start and end apart: 18 -> 0, of which waited for: 12 -> 0; matrix products, arithmetic and copies ran while one was open for 14% -> 0% of each run, Pallas kernels for 0% -> 0%
where the time goes in v2:
time: 128 us; the launch traced here: 127 us
  Pallas kernels  121 us (95%)
  local copies, waits for them, and re-layouts  4.12 us (3%)
  between operations  1.3 us (1%)
    pallas_call x1, Pallas kernels, per_device(): pl.pallas_call(functools.partial(kernel, lat_count, rad_count, blocks, ow...  121 us
    unnamed x4, local copies, waits for them, and re-layouts  2.91 us

profile of v2, /device:TPU:1, one launch (start us, length us, event | category | flops | bytes accessed | tf_op | source)
XLA Modules:
  0.0 127.3 jit_solution(12083171589021282935)
XLA Ops:
  1.3 1.8 %copy.8.positions = f32[128,3,128]{2,1,0:T(4,128)} copy(f32[128,3,128]{2,0,1:T(8,128)} %param.6) | data formatting | bytes 393216 | tf_op args[0]
  3.0 121.1 %advect.1 = (f32[192,8,128]{2,1,0:T(8,128)}, f32[512,256]{1,0:T(8,128)}) custom-call(s32[1]{0:T(128)S(6)} %copy.10.counts, s32[3,128]{1,0:T(4,128)} %elements.1, s32[2,128]{1,0:T(2,128)} %routes.1, f32[128,3,128]{2,1,0:T(4,128)} %copy.8.positions, bf16[128,16,128]{2,1,0:T(8,128)(2,1)} %fields.1, f32[81,256]{1,0:T(8,128)} %velocity.1), custom_call_target="tpu_custom_call" | custom-call | tf_op jit(solution)/shard_map/advect/pallas_call | solution.py:285
  124.1 1.2 slice.9
  125.3 0.0 copy-start
  125.3 0.7 copy.9
  126.1 0.4 copy-done
  126.5 0.8 broadcast_divide_fusion
  (2 shorter events, 0.0 us)
Async XLA Ops:
  125.3 1.1 copy-start

commit v3 on v2

v3 whole, which is shorter than its diff:
```python
import functools

import jax
import jax.numpy as jnp
from jax import lax
from jax.experimental import pallas as pl
from jax.experimental.pallas import tpu as pltpu
from jax.sharding import PartitionSpec as P

time_step = 0.4
MESH = pl.DeviceIdType.MESH
LANES = 128
GROUP = 8
NX, NY, NC = 4, 8, 2
NODES = 27
COLUMNS = 3 * NODES
ASKED, ROUTE = 81, 82
WEIGHTS, TAG = 48, 127
CHUNKS = ((3, 0), (1, 2))
NT = (((1,), (1,)), ((), ()))


def product(a, b, dims=(((1,), (0,)), ((), ()))):
    return lax.dot_general(a, b, dims, preferred_element_type=jnp.float32)


def halves(x, axis):
    high = x.astype(jnp.bfloat16)
    return jnp.concatenate([high, (x - high.astype(jnp.float32)).astype(jnp.bfloat16)], axis=axis)


def iota(shape, axis):
    return lax.broadcasted_iota(jnp.int32, shape, axis)


def onehot(mask):
    return jnp.where(mask, 1.0, 0.0).astype(jnp.bfloat16)


def lagrange(s):
    return 2.0 * (s - 0.5) * (s - 1.0), -4.0 * s * (s - 1.0), 2.0 * s * (s - 0.5)


def speed(coefficient, points):
    along = [lagrange(p) for p in points]
    result = []
    for c in range(3):
        total = None
        for i in range(3):
            plane = None
            for j in range(3):
                line = None
                for k in range(3):
                    term = coefficient(c * NODES + 9 * i + 3 * j + k) * along[2][k]
                    line = term if line is None else line + term
                line = line * along[1][j]
                plane = line if plane is None else plane + line
            plane = plane * along[0][i]
            total = plane if total is None else total + plane
        result.append(total)
    return result


def basis(points):
    along = [lagrange(p) for p in points]
    shapes = []
    for i in range(3):
        for j in range(3):
            both = along[0][i] * along[1][j]
            for k in range(3):
                shapes.append(both * along[2][k])
    return shapes


def kernel(
    lat_count, rad_count, blocks, owned,
    counts, elements, routes, positions, fields, velocity,
    moved, totals,
    raw, pos, fld, vel, posT, midT, lndT, lnd, mom, wts, colT, repT, midcol, midrep, midpos, midlnd,
    req_s, req_r, rep_s, rep_r, pos_s, pos_r, lnd_s, one_s, one_r, two_s, two_r,
    load_sems, self_sem, send_sems, recv_sems,
):
    lat = lax.axis_index("lat")
    rad = lax.axis_index("rad")
    places = 3 * rad_count
    mine = rad_count + rad
    x0, y0, c0 = rad // (NY * NC), lax.rem(rad // NC, NY), lax.rem(rad, NC)

    def lat_at(shift):
        return lax.rem(lat + shift + lat_count, lat_count)

    def over_partners(act, back=False):
        lats = [lat_at((1 - k) if back else (k - 1)) for k in range(3)]

        def step(j, carry):
            for m in reversed(range(NY)):
                dy = ((m + 1) // 2 if m % 2 else NY - (m + 1) // 2) % NY
                x = lax.rem(x0 + j // NC + m % NX, NX)
                y = lax.rem(y0 + dy, NY)
                q = (x * NY + y) * NC + lax.rem(c0 + j, NC)
                for k in range(3):
                    if k == 1 and m == 0:
                        @pl.when(j != 0)
                        def _():
                            act(k, q, (lats[k], q))
                    else:
                        act(k, q, (lats[k], q))
            return carry

        lax.fori_loop(0, NX * NC, step, 0)

    def send(source, target, number, rows, back=False):
        local = pltpu.make_async_copy(
            source.at[mine, pl.ds(0, rows)], target.at[mine, pl.ds(0, rows)], self_sem
        )
        local.start()

        def act(k, q, device):
            pltpu.make_async_remote_copy(
                src_ref=source.at[k * rad_count + q, pl.ds(0, rows)],
                dst_ref=target.at[k * rad_count + rad, pl.ds(0, rows)],
                send_sem=send_sems.at[number], recv_sem=recv_sems.at[number],
                device_id=device, device_id_type=MESH,
            ).start()

        over_partners(act, back)
        local.wait()

    def settle(buffer, sems, number, rows):
        span = buffer.at[pl.ds(0, places - 1), pl.ds(0, rows)]
        pltpu.make_async_copy(span, span, sems.at[number]).wait()

    loads = [
        pltpu.make_async_copy(velocity, raw, load_sems.at[0]),
        pltpu.make_async_copy(positions, pos, load_sems.at[1]),
        pltpu.make_async_copy(fields, fld, load_sems.at[2]),
    ]
    for load in loads:
        load.start()
    barrier = pltpu.get_barrier_semaphore()
    over_partners(
        lambda k, q, device: pl.semaphore_signal(barrier, inc=1, device_id=device, device_id_type=MESH)
    )

    def groups(count, size, act, unroll=1):
        def step(g, carry):
            act(pl.ds(pl.multiple_of(g * size, size), size))
            return carry

        lax.fori_loop(0, count // size, step, 0, unroll=unroll)

    live = iota((1, blocks), 1) < counts[0]
    element = elements[...]
    route = routes[...]
    first_route = jnp.where(live, route[0:1], -1)
    to_place = onehot(iota((places, blocks), 0) == first_route)
    twice = jnp.concatenate([to_place, to_place], axis=1)
    loads[0].wait()
    vel[pl.ds(80, 48), :] = jnp.zeros((48, owned), jnp.float32)
    vel[pl.ds(0, COLUMNS), :] = raw[...]
    columns = halves(vel[...], 0)
    start_hits = onehot(iota((owned, blocks), 0) == element[0:1])
    row = iota((LANES, blocks), 0)
    labels = jnp.where(row == ASKED, element[1:2] + 1, jnp.where(row == ROUTE, route[1:2], 0))
    both = product(columns, start_hits)
    colT[...] = both[:LANES] + both[LANES:] + labels.astype(jnp.float32)
    req_s[:, 0, :] = product(twice, halves(colT[...], 1), NT)
    loads[1].wait()
    for c in range(3):
        pos_s[:, c, :] = product(twice, halves(pos[c], 0))
    pl.semaphore_wait(barrier, places - 1)
    send(req_s, req_r, 0, 1)
    send(pos_s, pos_r, 2, 3)

    for c in range(3):
        posT[c] = pos[c].T

    def first_step(rows):
        points = [posT[c, rows, :] for c in range(3)]
        for c, u in enumerate(speed(lambda n: colT[pl.ds(n, 1), :], points)):
            midT[c, rows, :] = points[c] + 0.5 * time_step * u

    groups(LANES, 16, first_step, 2)

    settle(req_r, recv_sems, 0, 1)
    asked = req_r[:, 0, :]
    middle_hits = onehot(iota((places, owned), 1) == asked[:, ASKED : ASKED + 1].astype(jnp.int32) - 1)
    both = product(middle_hits, columns, NT)
    reply = both[:, :LANES] + both[:, LANES:]
    rep_s[:, 0, :] = reply
    send(rep_s, rep_r, 1, 1, back=True)
    midrep[...] = reply.T
    midcol[...] = asked.T
    second_route = jnp.where(
        midcol[pl.ds(ASKED, 1), :] > 0.5, midcol[pl.ds(ROUTE, 1), :].astype(jnp.int32), -1
    )
    to_final = onehot(iota((places, places), 0) == second_route)
    loads[2].wait()

    settle(pos_r, recv_sems, 2, 3)
    for c in range(3):
        midpos[c] = pos_r[:, c, :].T

    def middle_step(rows):
        points = [midpos[c, rows, :] for c in range(3)]
        first = speed(lambda n: midcol[pl.ds(n, 1), :], points)
        halfway = [points[c] + 0.5 * time_step * first[c] for c in range(3)]
        second = speed(lambda n: midrep[pl.ds(n, 1), :], halfway)
        for c in range(3):
            midlnd[c, rows, :] = points[c] + time_step * second[c]

    groups(LANES, GROUP, middle_step, 2)
    for c in range(3):
        both = product(to_final, halves(midlnd[c], 0), NT)
        lnd_s[:, c, :] = both[:, :LANES] + both[:, LANES:]
    send(lnd_s, moved, 7, 3)

    settle(rep_r, recv_sems, 1, 1)
    both = product(halves(rep_r[:, 0, :].T, 0), to_place)
    repT[...] = both[:LANES] + both[LANES:]

    def second_step(rows):
        points = [midT[c, rows, :] for c in range(3)]
        for c, u in enumerate(speed(lambda n: repT[pl.ds(n, 1), :], points)):
            lndT[c, rows, :] = posT[c, rows, :] + time_step * u

    groups(LANES, 16, second_step, 2)
    for c in range(3):
        lnd[c] = lndT[c].T

    lane = iota((GROUP, LANES), 1)
    own = lane // 16 == iota((GROUP, LANES), 0)
    odd = [(iota((GROUP, LANES), 0) // (1 << bit)) % 2 == 1 for bit in range(3)]

    def moment_step(rows):
        shapes = halves(jnp.concatenate(basis([lnd[c, rows, :] for c in range(3)]), axis=0), 1)
        block_fields = fld[rows].reshape(GROUP * 16, LANES)
        crossed = product(shapes, jnp.concatenate([block_fields, block_fields], axis=1), NT)
        for r in range(4):
            total = None
            for n in range(8 * r, min(8 * r + 8, NODES)):
                part = jnp.where(own, crossed[n * GROUP : (n + 1) * GROUP], 0.0)
                part = pltpu.roll(part, 16 * (n - 8 * r), 1) if n % 8 else part
                total = part if total is None else total + part
            for bit in range(3):
                total = jnp.where(odd[bit], pltpu.roll(total, LANES - (16 << bit), 1), total)
            mom[r, rows, :] = total

    groups(blocks, GROUP, moment_step, 4)

    def weight_step(g, sums):
        rows = pl.ds(pl.multiple_of(g * GROUP, GROUP), GROUP)
        squares = [[v * v for v in lagrange(lndT[c, rows, :])] for c in range(3)]
        result = []
        for i in range(3):
            for j in range(3):
                pair = squares[0][i] * squares[1][j]
                for k in range(3):
                    result.append(sums[len(result)] + pair * squares[2][k])
        return tuple(result)

    sums = lax.fori_loop(
        0, LANES // GROUP, weight_step, tuple(jnp.zeros((GROUP, blocks), jnp.float32) for _ in range(NODES)),
        unroll=2,
    )
    wts[...] = jnp.where(row == TAG, element[2:3] + 1, 0).astype(jnp.float32)
    for n in range(NODES):
        wts[pl.ds(WEIGHTS + n, 1), :] = jnp.sum(sums[n], axis=0, keepdims=True)
    mom[3] = mom[3] + wts[...].T

    for number, chunk in enumerate(CHUNKS):
        placed = product(twice, halves(jnp.concatenate([mom[r] for r in chunk], axis=1), 0))
        for place in range(len(chunk)):
            one_s[number, :, place, :] = placed[:, place * LANES : (place + 1) * LANES]
        send(one_s.at[number], one_r.at[number], 3 + number, len(chunk))

    for number, chunk in enumerate(CHUNKS):
        settle(one_r.at[number], recv_sems, 3 + number, len(chunk))
        wide = len(chunk) * LANES
        arrived = jnp.concatenate([one_r[number, :, place, :] for place in range(len(chunk))], axis=1)
        both = product(to_final, halves(arrived, 1))
        both = both[:, :wide] + both[:, wide:]
        for place in range(len(chunk)):
            two_s[number, :, place, :] = both[:, place * LANES : (place + 1) * LANES]
        send(two_s.at[number], two_r.at[number], 5 + number, len(chunk))

    hits = None
    for number, chunk in enumerate(CHUNKS):
        settle(two_r.at[number], recv_sems, 5 + number, len(chunk))
        if hits is None:
            tag = two_r[number, :, 0, :][:, TAG : TAG + 1].astype(jnp.int32) - 1
            hits = onehot(iota((places, owned), 1) == tag)
        wide = len(chunk) * LANES
        arrived = jnp.concatenate([two_r[number, :, place, :] for place in range(len(chunk))], axis=1)
        both = product(halves(arrived.T, 0), hits)
        both = both[:wide] + both[wide:]
        for place, r in enumerate(chunk):
            totals[pl.ds(r * LANES, LANES), :] = both[place * LANES : (place + 1) * LANES]
    settle(moved, recv_sems, 7, 3)
    for number, (buffer, rows) in enumerate(
        [(req_r, 1), (rep_r, 1), (pos_r, 3), (one_r.at[0], 2), (one_r.at[1], 2), (two_r.at[0], 2), (two_r.at[1], 2), (moved, 3)]
    ):
        settle(buffer, send_sems, number, rows)


def per_device(positions, fields, velocity, counts, elements, routes):
    lat_count, rad_count = lax.axis_size("lat"), lax.axis_size("rad")
    places = 3 * rad_count
    blocks = positions.shape[0]
    owned = velocity.shape[1]
    buffer = pltpu.VMEM((places, 8, LANES), jnp.float32)
    pair = pltpu.VMEM((2, places, 8, LANES), jnp.float32)
    square = pltpu.VMEM((blocks, LANES), jnp.float32)
    square3 = pltpu.VMEM((3, blocks, LANES), jnp.float32)
    vmem = pl.BlockSpec(memory_space=pltpu.VMEM)
    anywhere = pl.BlockSpec(memory_space=pl.ANY)
    moved, totals = pl.pallas_call(
        functools.partial(kernel, lat_count, rad_count, blocks, owned),
        out_shape=[
            jax.ShapeDtypeStruct((places, 8, LANES), jnp.float32),
            jax.ShapeDtypeStruct((4 * LANES, owned), jnp.float32),
        ],
        in_specs=[pl.BlockSpec(memory_space=pltpu.SMEM), vmem, vmem, anywhere, anywhere, anywhere],
        out_specs=[vmem, vmem],
        scratch_shapes=[
            pltpu.VMEM(velocity.shape, jnp.float32),
            square3,
            pltpu.VMEM(fields.shape, fields.dtype),
            pltpu.VMEM((LANES, owned), jnp.float32),
            square3, square3, square3, square3,
            pltpu.VMEM((4, blocks, LANES), jnp.float32),
            square, square, square,
            pltpu.VMEM((LANES, places), jnp.float32),
            pltpu.VMEM((LANES, places), jnp.float32),
            pltpu.VMEM((3, LANES, places), jnp.float32),
            pltpu.VMEM((3, LANES, places), jnp.float32),
            buffer, buffer, buffer, buffer, buffer, buffer, buffer, pair, pair, pair, pair,
            pltpu.SemaphoreType.DMA((3,)),
            pltpu.SemaphoreType.DMA,
            pltpu.SemaphoreType.DMA((8,)),
            pltpu.SemaphoreType.DMA((8,)),
        ],
        compiler_params=pltpu.CompilerParams(collective_id=0, has_side_effects=True),
        name="advect",
    )(counts, elements, routes, jnp.transpose(positions, (1, 0, 2)), fields, velocity)
    weights = totals[3 * LANES + WEIGHTS : 3 * LANES + WEIGHTS + NODES]
    projected = totals[: NODES * 16].reshape(NODES, 16, owned) / (1.0 + weights[:, None, :])
    return moved[:, :3], projected


def solution(mesh):
    in_specs = (
        P(("lat", "rad"), None, None),
        P(("lat", "rad"), None, None),
        P(None, ("lat", "rad")),
        P(("lat", "rad")),
        P(None, ("lat", "rad")),
        P(None, ("lat", "rad")),
    )
    out_specs = (P(("lat", "rad"), None, None), P(None, None, ("lat", "rad")))
    return jax.shard_map(
        per_device, mesh=mesh, in_specs=in_specs, out_specs=out_specs, check_vma=False
    )
```

time: 128 us -> 76.1 us (0.59)
  Pallas kernels: 121 us -> 71.4 us
  local copies, waits for them, and re-layouts: 4.12 us -> 2.36 us
    pallas_call x1, Pallas kernels: 121 us -> 71.4 us  [per_device(): pl.pallas_call(functools.partial(kernel, lat_count, rad_count, blocks, ow...]
    unnamed x4 -> x3, local copies, waits for them, and re-layouts: 2.91 us -> 1.14 us
where the time goes in v3:
time: 76.1 us; the launch traced here: 75.9 us
  Pallas kernels  71.4 us (94%)
  local copies, waits for them, and re-layouts  2.36 us (3%)
  between operations  1.3 us (2%)
  other arithmetic  0.81 us (1%)
    pallas_call x1, Pallas kernels, per_device(): pl.pallas_call(functools.partial(kernel, lat_count, rad_count, blocks, ow...  71.4 us

profile of v3, /device:TPU:1, one launch (start us, length us, event | category | flops | bytes accessed | tf_op | source)
XLA Modules:
  0.0 75.9 jit_solution(11783181615701822228)
XLA Ops:
  1.3 71.4 %advect.1 = (f32[192,8,128]{2,1,0:T(8,128)}, f32[512,256]{1,0:T(8,128)}) custom-call(s32[1]{0:T(128)S(6)} %copy.9.counts, s32[3,128]{1,0:T(4,128)} %elements.1, s32[2,128]{1,0:T(2,128)} %routes.1, f32[3,128,128]{2,1,0:T(8,128)} %bitcast.3, bf16[128,16,128]{2,1,0:T(8,128)(2,1)} %fields.1, f32[81,256]{1,0:T(8,128)} %velocity.1), custom_call_target="tpu_custom_call" | custom-call | tf_op jit(solution)/shard_map/advect/pallas_call | solution.py:317
  72.7 1.2 %slice.9 = f32[192,3,128]{2,1,0:T(4,128)S(1)} slice(f32[192,8,128]{2,1,0:T(8,128)} %get-tuple-element.4), slice={[0:192], [0:3], [0:128]} | slice | bytes 589824 | tf_op jit(solution)/shard_map/slice | solution.py:348
  73.9 0.0 copy-start
  73.9 0.7 copy.8
  74.6 0.4 copy-done
  75.1 0.8 %broadcast_divide_fusion = f32[27,16,256]{2,1,0:T(8,128)} fusion(f32[27,16,256]{2,1,0:T(8,128)S(1)} %bitcast.2, f32[27,256]{1,0:T(8,128)S(1)} %slice_add_fusion), kind=kLoop, calls=%fused_computation | loop fusion | flops 110592 | bytes 912384 | tf_op jit(solution)/shard_map/div | solution.py:347
  (2 shorter events, 0.0 us)
Async XLA Ops:
  73.9 1.1 %copy-start = (f32[512,256]{1,0:T(8,128)S(1)}, f32[512,256]{1,0:T(8,128)}, u32[]{:S(2)}) copy-start(f32[512,256]{1,0:T(8,128)} %get-tuple-element.5) | copy-start | bytes 1572868

commit v4 on v3

--- a/solution.py
+++ b/solution.py
@@ -16,7 +16,7 @@
 COLUMNS = 3 * NODES
 ASKED, ROUTE = 81, 82
 WEIGHTS, TAG = 48, 127
-CHUNKS = ((3, 0), (1, 2))
+CHUNKS = ((0, 1), (2, 3))
 NT = (((1,), (1,)), ((), ()))
 
 
@@ -74,8 +74,9 @@
 
 def kernel(
     lat_count, rad_count, blocks, owned,
-    counts, elements, routes, positions, fields, velocity,
-    moved, totals,
+    counts_hbm, elements_hbm, routes_hbm, positions, fields, velocity,
+    placed_out, projected,
+    moved, totals, counts, elements, routes,
     raw, pos, fld, vel, posT, midT, lndT, lnd, mom, wts, colT, repT, midcol, midrep, midpos, midlnd,
     req_s, req_r, rep_s, rep_r, pos_s, pos_r, lnd_s, one_s, one_r, two_s, two_r,
     load_sems, self_sem, send_sems, recv_sems,
@@ -90,13 +91,14 @@
         return lax.rem(lat + shift + lat_count, lat_count)
 
     def over_partners(act, back=False):
+        side = 1 - 2 * lax.rem(x0 + y0 + c0, 2)
         lats = [lat_at((1 - k) if back else (k - 1)) for k in range(3)]
 
         def step(j, carry):
             for m in reversed(range(NY)):
                 dy = ((m + 1) // 2 if m % 2 else NY - (m + 1) // 2) % NY
-                x = lax.rem(x0 + j // NC + m % NX, NX)
-                y = lax.rem(y0 + dy, NY)
+                x = lax.rem(x0 + side * lax.rem(j // NC + m % NX, NX) + NX, NX)
+                y = lax.rem(y0 + side * dy + NY, NY)
                 q = (x * NY + y) * NC + lax.rem(c0 + j, NC)
                 for k in range(3):
                     if k == 1 and m == 0:
@@ -130,18 +132,20 @@
         span = buffer.at[pl.ds(0, places - 1), pl.ds(0, rows)]
         pltpu.make_async_copy(span, span, sems.at[number]).wait()
 
+    barrier = pltpu.get_barrier_semaphore()
+    over_partners(
+        lambda k, q, device: pl.semaphore_signal(barrier, inc=1, device_id=device, device_id_type=MESH)
+    )
     loads = [
         pltpu.make_async_copy(velocity, raw, load_sems.at[0]),
         pltpu.make_async_copy(positions, pos, load_sems.at[1]),
         pltpu.make_async_copy(fields, fld, load_sems.at[2]),
+        pltpu.make_async_copy(counts_hbm, counts, load_sems.at[3]),
+        pltpu.make_async_copy(elements_hbm, elements, load_sems.at[4]),
+        pltpu.make_async_copy(routes_hbm, routes, load_sems.at[5]),
     ]
     for load in loads:
         load.start()
-    barrier = pltpu.get_barrier_semaphore()
-    over_partners(
-        lambda k, q, device: pl.semaphore_signal(barrier, inc=1, device_id=device, device_id_type=MESH)
-    )
-
     def groups(count, size, act, unroll=1):
         def step(g, carry):
             act(pl.ds(pl.multiple_of(g * size, size), size))
@@ -149,6 +153,8 @@
 
         lax.fori_loop(0, count // size, step, 0, unroll=unroll)
 
+    for load in loads[3:]:
+        load.wait()
     live = iota((1, blocks), 1) < counts[0]
     element = elements[...]
     route = routes[...]
@@ -232,21 +238,23 @@
     own = lane // 16 == iota((GROUP, LANES), 0)
     odd = [(iota((GROUP, LANES), 0) // (1 << bit)) % 2 == 1 for bit in range(3)]
 
-    def moment_step(rows):
-        shapes = halves(jnp.concatenate(basis([lnd[c, rows, :] for c in range(3)]), axis=0), 1)
-        block_fields = fld[rows].reshape(GROUP * 16, LANES)
-        crossed = product(shapes, jnp.concatenate([block_fields, block_fields], axis=1), NT)
-        for r in range(4):
-            total = None
-            for n in range(8 * r, min(8 * r + 8, NODES)):
-                part = jnp.where(own, crossed[n * GROUP : (n + 1) * GROUP], 0.0)
-                part = pltpu.roll(part, 16 * (n - 8 * r), 1) if n % 8 else part
-                total = part if total is None else total + part
-            for bit in range(3):
-                total = jnp.where(odd[bit], pltpu.roll(total, LANES - (16 << bit), 1), total)
-            mom[r, rows, :] = total
-
-    groups(blocks, GROUP, moment_step, 4)
+    def moment_steps(nodes):
+        def moment_step(rows):
+            every = basis([lnd[c, rows, :] for c in range(3)])
+            shapes = halves(jnp.concatenate([every[n] for n in nodes], axis=0), 1)
+            block_fields = fld[rows].reshape(GROUP * 16, LANES)
+            crossed = product(shapes, jnp.concatenate([block_fields, block_fields], axis=1), NT)
+            lines = {}
+            for place, n in enumerate(nodes):
+                part = jnp.where(own, crossed[place * GROUP : (place + 1) * GROUP], 0.0)
+                part = pltpu.roll(part, 16 * (n % 8), 1) if n % 8 else part
+                lines[n // 8] = lines[n // 8] + part if n // 8 in lines else part
+            for r, total in lines.items():
+                for bit in range(3):
+                    total = jnp.where(odd[bit], pltpu.roll(total, LANES - (16 << bit), 1), total)
+                mom[r, rows, :] = total
+
+        groups(blocks, GROUP, moment_step, 4)
 
     def weight_step(g, sums):
         rows = pl.ds(pl.multiple_of(g * GROUP, GROUP), GROUP)
@@ -259,16 +267,15 @@
                     result.append(sums[len(result)] + pair * squares[2][k])
         return tuple(result)
 
-    sums = lax.fori_loop(
-        0, LANES // GROUP, weight_step, tuple(jnp.zeros((GROUP, blocks), jnp.float32) for _ in range(NODES)),
-        unroll=2,
-    )
-    wts[...] = jnp.where(row == TAG, element[2:3] + 1, 0).astype(jnp.float32)
-    for n in range(NODES):
-        wts[pl.ds(WEIGHTS + n, 1), :] = jnp.sum(sums[n], axis=0, keepdims=True)
-    mom[3] = mom[3] + wts[...].T
-
     for number, chunk in enumerate(CHUNKS):
+        moment_steps([n for n in range(NODES) if n // 8 in chunk])
+        if 3 in chunk:
+            zeros = tuple(jnp.zeros((GROUP, blocks), jnp.float32) for _ in range(NODES))
+            sums = lax.fori_loop(0, LANES // GROUP, weight_step, zeros, unroll=2)
+            wts[...] = jnp.where(row == TAG, element[2:3] + 1, 0).astype(jnp.float32)
+            for n in range(NODES):
+                wts[pl.ds(WEIGHTS + n, 1), :] = jnp.sum(sums[n], axis=0, keepdims=True)
+            mom[3] = mom[3] + wts[...].T
         placed = product(twice, halves(jnp.concatenate([mom[r] for r in chunk], axis=1), 0))
         for place in range(len(chunk)):
             one_s[number, :, place, :] = placed[:, place * LANES : (place + 1) * LANES]
@@ -284,19 +291,25 @@
             two_s[number, :, place, :] = both[:, place * LANES : (place + 1) * LANES]
         send(two_s.at[number], two_r.at[number], 5 + number, len(chunk))
 
-    hits = None
+    settle(moved, recv_sems, 7, 3)
+    for c in range(3):
+        placed_out[c] = moved[:, c, :]
+    turned = []
     for number, chunk in enumerate(CHUNKS):
         settle(two_r.at[number], recv_sems, 5 + number, len(chunk))
-        if hits is None:
-            tag = two_r[number, :, 0, :][:, TAG : TAG + 1].astype(jnp.int32) - 1
-            hits = onehot(iota((places, owned), 1) == tag)
+        arrived = jnp.concatenate([two_r[number, :, place, :] for place in range(len(chunk))], axis=1)
+        turned.append(halves(arrived.T, 0))
+    tag = two_r[1, :, CHUNKS[1].index(3), :][:, TAG : TAG + 1].astype(jnp.int32) - 1
+    hits = onehot(iota((places, owned), 1) == tag)
+    for number, chunk in enumerate(CHUNKS):
         wide = len(chunk) * LANES
-        arrived = jnp.concatenate([two_r[number, :, place, :] for place in range(len(chunk))], axis=1)
-        both = product(halves(arrived.T, 0), hits)
+        both = product(turned[number], hits)
         both = both[:wide] + both[wide:]
         for place, r in enumerate(chunk):
             totals[pl.ds(r * LANES, LANES), :] = both[place * LANES : (place + 1) * LANES]
-    settle(moved, recv_sems, 7, 3)
+    for n in range(NODES):
+        weight = totals[pl.ds(3 * LANES + WEIGHTS + n, 1), :]
+        projected[pl.ds(16 * n, 16), :] = totals[pl.ds(16 * n, 16), :] / (1.0 + weight)
     for number, (buffer, rows) in enumerate(
         [(req_r, 1), (rep_r, 1), (pos_r, 3), (one_r.at[0], 2), (one_r.at[1], 2), (two_r.at[0], 2), (two_r.at[1], 2), (moved, 3)]
     ):
@@ -314,15 +327,20 @@
     square3 = pltpu.VMEM((3, blocks, LANES), jnp.float32)
     vmem = pl.BlockSpec(memory_space=pltpu.VMEM)
     anywhere = pl.BlockSpec(memory_space=pl.ANY)
-    moved, totals = pl.pallas_call(
+    placed, projected = pl.pallas_call(
         functools.partial(kernel, lat_count, rad_count, blocks, owned),
         out_shape=[
-            jax.ShapeDtypeStruct((places, 8, LANES), jnp.float32),
-            jax.ShapeDtypeStruct((4 * LANES, owned), jnp.float32),
+            jax.ShapeDtypeStruct((3, places, LANES), jnp.float32),
+            jax.ShapeDtypeStruct((NODES * 16, owned), jnp.float32),
         ],
-        in_specs=[pl.BlockSpec(memory_space=pltpu.SMEM), vmem, vmem, anywhere, anywhere, anywhere],
+        in_specs=[anywhere] * 6,
         out_specs=[vmem, vmem],
         scratch_shapes=[
+            buffer,
+            pltpu.VMEM((4 * LANES, owned), jnp.float32),
+            pltpu.SMEM((1,), jnp.int32),
+            pltpu.VMEM(elements.shape, jnp.int32),
+            pltpu.VMEM(routes.shape, jnp.int32),
             pltpu.VMEM(velocity.shape, jnp.float32),
             square3,
             pltpu.VMEM(fields.shape, fields.dtype),
@@ -335,7 +353,7 @@
             pltpu.VMEM((3, LANES, places), jnp.float32),
             pltpu.VMEM((3, LANES, places), jnp.float32),
             buffer, buffer, buffer, buffer, buffer, buffer, buffer, pair, pair, pair, pair,
-            pltpu.SemaphoreType.DMA((3,)),
+            pltpu.SemaphoreType.DMA((6,)),
             pltpu.SemaphoreType.DMA,
             pltpu.SemaphoreType.DMA((8,)),
             pltpu.SemaphoreType.DMA((8,)),
@@ -343,9 +361,7 @@
         compiler_params=pltpu.CompilerParams(collective_id=0, has_side_effects=True),
         name="advect",
     )(counts, elements, routes, jnp.transpose(positions, (1, 0, 2)), fields, velocity)
-    weights = totals[3 * LANES + WEIGHTS : 3 * LANES + WEIGHTS + NODES]
-    projected = totals[: NODES * 16].reshape(NODES, 16, owned) / (1.0 + weights[:, None, :])
-    return moved[:, :3], projected
+    return jnp.transpose(placed, (1, 0, 2)), projected.reshape(NODES, 16, owned)
 
 
 def solution(mesh):

time: 76.1 us -> 74.1 us (0.974)
  Pallas kernels: 71.4 us -> 70.1 us
  other arithmetic: 0.81 us -> 0 us
    unnamed x3 -> x4, local copies, waits for them, and re-layouts: 1.14 us -> 2.51 us
    pallas_call x1, Pallas kernels: 71.4 us -> 70.1 us  [per_device(): pl.pallas_call(functools.partial(kernel, lat_count, rad_count, blocks, ow...]
    slice x2 -> x0, local copies, waits for them, and re-layouts: 1.21 us -> none  [the longest x1 1.19 us: per_device(): return (moved[:, :3], projected)]
    div x1 -> x0, other arithmetic: 0.81 us -> none  [per_device(): totals[:NODES * 16].reshape(NODES, 16, owned) / (1.0 + weights[:, None, :])]
where the time goes in v4:
time: 74.1 us; the launch traced here: 73.9 us
  Pallas kernels  70.1 us (95%)
  local copies, waits for them, and re-layouts  2.51 us (3%)
  between operations  1.29 us (2%)
    pallas_call x1, Pallas kernels, per_device(): pl.pallas_call(functools.partial(kernel, lat_count, rad_count, blocks, ow...  70.1 us
    unnamed x4, local copies, waits for them, and re-layouts  2.51 us

profile of v4, /device:TPU:1, one launch (start us, length us, event | category | flops | bytes accessed | tf_op | source)
XLA Modules:
  0.0 73.9 jit_solution(8636914839140657516)
XLA Ops:
  1.3 70.1 %advect.1 = (f32[3,192,128]{2,1,0:T(8,128)}, f32[432,256]{1,0:T(8,128)}) custom-call(s32[1]{0:T(128)S(6)} %copy.10.counts_hbm, s32[3,128]{1,0:T(4,128)} %elements_hbm.1, s32[2,128]{1,0:T(2,128)} %routes_hbm.1, f32[3,128,128]{2,1,0:T(8,128)} %bitcast.5, bf16[128,16,128]{2,1,0:T(8,128)(2,1)} %fields.1, f32[81,256]{1,0:T(8,128)} %velocity.1), custom_call_target="tpu_custom_call" | custom-call | tf_op jit(solution)/shard_map/advect/pallas_call | solution.py:330
  71.4 0.0 copy-start
  71.4 1.7 %copy.11 = f32[192,3,128]{2,0,1:T(8,128)} copy(f32[192,3,128]{2,0,1:T(8,128)} %bitcast.4) | data formatting | bytes 589824
  73.1 0.0 copy-done
  73.1 0.8 %copy.12 = f32[27,16,256]{2,1,0:T(8,128)} copy(f32[27,16,256]{2,1,0:T(8,128)S(1)} %bitcast.3) | data formatting | bytes 884736
Async XLA Ops:
  71.4 1.8 %copy-start = (f32[432,256]{1,0:T(8,128)S(1)}, f32[432,256]{1,0:T(8,128)}, u32[]{:S(2)}) copy-start(f32[432,256]{1,0:T(8,128)} %get-tuple-element.5) | copy-start | bytes 1327108
